TPU v7x, 256 devices: a whole 4x4x8 slice. The times are simulated.
256 devices in a mesh: sub: 64 (over y, z, x_lo), iter: 4 (over x_hi, core).
Axes of the slice: x: 4 (x_hi: 2, x_lo: 2; x = x_hi * 2 + x_lo), y: 4, z: 8, core: 2. Of those that a mesh axis runs over, the one named last changes fastest.
Arguments:
- fields: float32 [4, 128, 128, 128], P('iter', 'sub'), may hold values from -6 to 6
- labels: int32 [128, 128, 128], P('sub'), may hold values from 0 to 3
- traces: float32 [4, 64, 4, 128, 128], P('iter', 'sub'), may hold values from -6 to 6
- new_guess: float32 [2, 64, 4, 128, 128], P(None, 'sub'), may hold values from -6 to 6
- cond_table: float32 [4], replicated, may hold values from 0.2 to 5
- cap_table: float32 [4], replicated, may hold values from 0.5 to 4
Outputs:
- end_fields: float32 [4, 128, 128, 128], P('iter', 'sub')
- corrected: float32 [4, 64, 4, 128, 128], P('iter', 'sub')
All inputs are finite; a program needn't handle non-finite values.
Results may differ from a plain program's by a relative error of at most 0.00002.
Values sent between devices are 32-bit elements; how exact they have to be, the bound alone decides.
A program may use at most 64 MiB of HBM per device.

v0:
```python
import jax
import jax.numpy as jnp
from jax import lax
from jax.sharding import PartitionSpec as P

SWEEPS = 3
TICKS = 3


def shifted(value, axis, steps):
    count = lax.axis_size(axis)
    leading, last = (max(0, -steps), min(count, count - steps))
    return lax.ppermute(value, axis, [(source, source + steps) for source in range(leading, last)])


def harmonic(first, second):
    return 2.0 * first * second / (first + second)


def setup(labels, cond_table, cap_table, left_mask, right_mask):
    conduct = jnp.zeros(labels.shape, jnp.float32)
    capacity = jnp.zeros(labels.shape, jnp.float32)
    for cls in range(cond_table.shape[0]):
        hit = labels == cls
        conduct = jnp.where(hit, cond_table[cls], conduct)
        capacity = jnp.where(hit, cap_table[cls], capacity)
    face_x = harmonic(conduct[:, 1:], conduct[:, :-1])
    face_y = harmonic(conduct[:, :, 1:], conduct[:, :, :-1])
    face_z = harmonic(conduct[:, :, :, 1:], conduct[:, :, :, :-1])
    end_first = 2.0 * conduct[:, 0]
    end_last = 2.0 * conduct[:, -1]
    sum_x = jnp.pad(face_x, ((0, 0), (1, 0), (0, 0), (0, 0))) + jnp.pad(
        face_x, ((0, 0), (0, 1), (0, 0), (0, 0))
    )
    sum_x = sum_x.at[:, 0].add(end_first).at[:, -1].add(end_last)
    sum_y = jnp.pad(face_y, ((0, 0), (0, 0), (1, 0), (0, 0))) + jnp.pad(
        face_y, ((0, 0), (0, 0), (0, 1), (0, 0))
    )
    sum_y = sum_y.at[:, :, 0].add(2.0 * conduct[:, :, 0]).at[:, :, -1].add(2.0 * conduct[:, :, -1])
    sum_z = jnp.pad(face_z, ((0, 0), (0, 0), (0, 0), (1, 0))) + jnp.pad(
        face_z, ((0, 0), (0, 0), (0, 0), (0, 1))
    )
    sum_z = (
        sum_z.at[:, :, :, 0]
        .add(2.0 * conduct[:, :, :, 0])
        .at[:, :, :, -1]
        .add(2.0 * conduct[:, :, :, -1])
    )
    diag_d = capacity + sum_x + sum_y + sum_z
    diag_n = diag_d.at[:, 0].add(-left_mask[:, None, None] * end_first)
    diag_n = diag_n.at[:, -1].add(-right_mask[:, None, None] * end_last)
    return (capacity, face_x, face_y, face_z, end_first, end_last, diag_d, diag_n)


def relax(value, rhs, diag, face_x, face_y, face_z):
    for sweep in range(SWEEPS):
        near = jnp.pad(face_x * value[:, :-1], ((0, 0), (1, 0), (0, 0), (0, 0)))
        near = near + jnp.pad(face_x * value[:, 1:], ((0, 0), (0, 1), (0, 0), (0, 0)))
        near = near + jnp.pad(face_y * value[:, :, :-1], ((0, 0), (0, 0), (1, 0), (0, 0)))
        near = near + jnp.pad(face_y * value[:, :, 1:], ((0, 0), (0, 0), (0, 1), (0, 0)))
        near = near + jnp.pad(face_z * value[:, :, :, :-1], ((0, 0), (0, 0), (0, 0), (1, 0)))
        near = near + jnp.pad(face_z * value[:, :, :, 1:], ((0, 0), (0, 0), (0, 0), (0, 1)))
        value = (rhs + near) / diag
    return value


def dirichlet(state, left_trace, right_trace, coeffs):
    capacity, face_x, face_y, face_z, end_first, end_last, diag_d, diag_n = coeffs
    firsts = []
    lasts = []
    for step in range(left_trace.shape[1]):
        rhs = capacity * state
        rhs = rhs.at[:, 0].add(end_first * left_trace[:, step])
        rhs = rhs.at[:, -1].add(end_last * right_trace[:, step])
        state = relax(state, rhs, diag_d, face_x, face_y, face_z)
        firsts.append(state[:, 0])
        lasts.append(state[:, -1])
    return (state, jnp.stack(firsts, axis=1), jnp.stack(lasts, axis=1))


def neumann(left_jump, right_jump, coeffs):
    capacity, face_x, face_y, face_z, end_first, end_last, diag_d, diag_n = coeffs
    psi = jnp.zeros(diag_n.shape, jnp.float32)
    firsts = []
    lasts = []
    for step in range(left_jump.shape[1]):
        rhs = capacity * psi
        rhs = rhs.at[:, 0].add(left_jump[:, step])
        rhs = rhs.at[:, -1].add(right_jump[:, step])
        psi = relax(psi, rhs, diag_n, face_x, face_y, face_z)
        firsts.append(psi[:, 0])
        lasts.append(psi[:, -1])
    return (jnp.stack(firsts, axis=1), jnp.stack(lasts, axis=1))


def local(fields, labels, traces, new_guess, cond_table, cap_table):
    sub_count = lax.axis_size("sub")
    sub_pos = lax.axis_index("sub")
    group_pos = lax.axis_index("iter")
    left_mask = jnp.reshape((sub_pos > 0).astype(jnp.float32), (1,))
    right_mask = jnp.reshape((sub_pos < sub_count - 1).astype(jnp.float32), (1,))
    right_wide = right_mask[:, None, None, None]
    coeffs = setup(labels[None], cond_table, cap_table, left_mask, right_mask)
    end_first, end_last = (coeffs[4], coeffs[5])
    state = fields
    right_trace = traces[0] * right_wide
    corrected = right_trace
    for tick in range(TICKS):
        left_trace = shifted(right_trace, "sub", 1)
        state, firsts, lasts = dirichlet(state, left_trace, right_trace, coeffs)
        q_first = end_first[:, None] * (firsts - left_trace)
        q_last = end_last[:, None] * (lasts - right_trace)
        from_right = shifted(q_first, "sub", -1)
        right_jump = (q_last + from_right) * right_wide
        left_jump = shifted(right_jump, "sub", 1)
        psi_first, psi_last = neumann(left_jump, right_jump, coeffs)
        psi_right = shifted(psi_first, "sub", -1)
        corrected = (right_trace + 0.25 * (psi_last + psi_right)) * right_wide
        if tick + 1 < TICKS:
            passed = shifted(corrected, "iter", 1)
            right_trace = jnp.where(group_pos == 0, new_guess[tick] * right_wide, passed)
    return (state, corrected[None])


def solution(mesh):
    return jax.shard_map(
        local,
        mesh=mesh,
        in_specs=(
            P("iter", "sub", None, None),
            P("sub", None, None),
            P("iter", "sub", None, None, None),
            P(None, "sub", None, None, None),
            P(),
            P(),
        ),
        out_specs=(P("iter", "sub", None, None), P("iter", "sub", None, None, None)),
        check_vma=False,
    )
```

profile of v0, /device:TPU:12, one launch (start us, length us, event | category | flops | bytes accessed | tf_op | source)
XLA Modules:
  0.0 234.0 jit_solution(16001611543618006104)
XLA Ops:
  0.7 1.0 multiply_bitcast_fusion
  1.7 3.1 %collective-permute-start = (f32[1,4,128,128]{3,2,1,0:T(8,128)S(1)}, f32[1,4,128,128]{3,2,1,0:T(8,128)S(1)}, u32[]{:S(2)}, u32[]{:S(2)}) collective-permute-start(f32[1,4,128,128]{3,2,1,0:T(8,128)S(1)} %multiply_bitcast_fusion), channel_id=1, source_target_pairs={{0,4},{4,8},{8,12},{12,16},{16,20},{20,24},{24,28},{28,32},{32,36}... | collective-permute-start | bytes 786440 | tf_op jit(solution)/shard_map/ppermute | solution.py:13
  4.8 0.6 fusion.124
  5.4 0.7 fusion.125
  6.1 2.6 %broadcast_multiply_fusion.2 = (f32[2,128,128]{2,1,0:T(8,128)S(1)}, pred[2,128,128]{2,1,0:T(8,128)(4,1)S(1)}, pred[2,128,128]{2,1,0:T(8,128)(4,1)S(1)}, pred[2,1...) fusion(f32[]{:T(128)} %bitcast.3, f32[]{:T(128)} %bitcast.2, f32[]{:T(128)} %bitcast.1, f32[]{:T(128)} %bitcast, ...), kind=kLoop, calls=%fused_computation.656 | loop fusion | flops 294912 | bytes 393232 | tf_op jit(solution)/shard_map/mul | solution.py:87
  8.7 5.0 %fusion.107 = (f32[1,2,128,128]{3,2,1,0:T(8,128)S(1)}, f32[1,2,128,128]{3,2,1,0:T(8,128)S(1)}) fusion(pred[2,128,128]{2,1,0:T(8,128)(4,1)S(1)} %get-tuple-element.718, pred[2,128,128]{2,1,0:T(8,128)(4,1)S(1)} %get-tuple-element.717, pred[2,128,128]{2,1,0:T(8,128)(4,1)S(1)} %get-tuple-element.716, pred[2,128,128]{2,1,0:T(8,128)(4,1)S(1)} %get-tuple-element.715, ...), kind=kLoop, calls=%fused_computation.709 | loop fusion | flops 294912 | bytes 393248 | tf_op jit(solution)/shard_map/mul | solution.py:87
  14.2 0.9 copy-done
  15.2 0.3 scatter-add.196
  15.5 0.1 fusion.22
  15.7 0.5 scatter-add.199
  16.3 2.6 %pad_add_fusion = (f32[1,2,128,128]{3,2,1,0:T(8,128)S(1)}, f32[1,2,128,128]{3,2,1,0:T(8,128)S(1)}) fusion(f32[1,1,128,128]{3,2,1,0:T(8,128)S(1)} %get-tuple-element.709, f32[1,2,128,128]{3,2,1,0:T(8,128)S(1)} %copy-done, pred[2,128,128]{2,1,0:T(8,128)(4,1)S(1)} %get-tuple-element.718, pred[2,128,128]{2,1,0:T(8,128)(4,1)S(1)} %get-tuple-element.717, ...), kind=kLoop, calls=%fused_computation.38 | loop fusion | flops 196608 | bytes 589840 | tf_op jit(solution)/shard_map/add | solution.py:32
  19.0 2.7 %add_divide_fusion.71 = (f32[1,2,128,128]{3,2,1,0:T(8,128)S(1)}, f32[1,2,128,128]{3,2,1,0:T(8,128)S(1)}) fusion(f32[1,2,128,128]{3,2,1,0:T(8,128)S(1)} %get-tuple-element.1208, f32[1,2,128,127]{3,2,1,0:T(8,128)S(1)} %get-tuple-element.1004, f32[1,2,128,127]{3,2,1,0:T(8,128)S(1)} %get-tuple-element.1003, f32[1,2,127,128]{3,2,1,0:T(8,128)S(1)} %get-tuple-element.1002, ...), kind=kLoop, calls=%fused_computation.412 | loop fusion | flops 458752 | bytes 1568784 | tf_op jit(solution)/shard_map/div | solution.py:63
  22.1 2.7 %bitcast_multiply_fusion.19 = (f32[1,2,128,128]{3,2,1,0:T(8,128)S(1)}, f32[1,2,128,128]{3,2,1,0:T(8,128)S(1)}) fusion(pred[2,128,128]{2,1,0:T(8,128)(4,1)S(1)} %get-tuple-element.718, pred[2,128,128]{2,1,0:T(8,128)(4,1)S(1)} %get-tuple-element.717, pred[2,128,128]{2,1,0:T(8,128)(4,1)S(1)} %get-tuple-element.716, ...), kind=kLoop, calls=%fused_computation.335 | loop fusion | flops 393216 | bytes 1306640 | tf_op jit(solution)/shard_map/mul | solution.py:72
  25.6 2.7 %bitcast_multiply_fusion.18 = (f32[1,2,128,128]{3,2,1,0:T(8,128)S(1)}, f32[1,2,128,128]{3,2,1,0:T(8,128)S(1)}) fusion(pred[2,128,128]{2,1,0:T(8,128)(4,1)S(1)} %get-tuple-element.718, pred[2,128,128]{2,1,0:T(8,128)(4,1)S(1)} %get-tuple-element.717, pred[2,128,128]{2,1,0:T(8,128)(4,1)S(1)} %get-tuple-element.716, ...), kind=kLoop, calls=%fused_computation.334 | loop fusion | flops 393216 | bytes 1306640 | tf_op jit(solution)/shard_map/mul | solution.py:72
  29.0 2.7 %bitcast_multiply_fusion.17 = (f32[1,2,128,128]{3,2,1,0:T(8,128)S(1)}, f32[1,2,128,128]{3,2,1,0:T(8,128)S(1)}) fusion(pred[2,128,128]{2,1,0:T(8,128)(4,1)S(1)} %get-tuple-element.718, pred[2,128,128]{2,1,0:T(8,128)(4,1)S(1)} %get-tuple-element.717, pred[2,128,128]{2,1,0:T(8,128)(4,1)S(1)} %get-tuple-element.716, ...), kind=kLoop, calls=%fused_computation.333 | loop fusion | flops 393216 | bytes 1306640 | tf_op jit(solution)/shard_map/mul | solution.py:72
  32.5 2.7 %bitcast_multiply_fusion.16 = (f32[1,2,128,128]{3,2,1,0:T(8,128)S(1)}, f32[1,2,128,128]{3,2,1,0:T(8,128)S(1)}) fusion(pred[2,128,128]{2,1,0:T(8,128)(4,1)S(1)} %get-tuple-element.718, pred[2,128,128]{2,1,0:T(8,128)(4,1)S(1)} %get-tuple-element.717, pred[2,128,128]{2,1,0:T(8,128)(4,1)S(1)} %get-tuple-element.716, ...), kind=kLoop, calls=%fused_computation.332 | loop fusion | flops 393216 | bytes 1306640 | tf_op jit(solution)/shard_map/mul | solution.py:72
  35.2 7.2 %collective-permute-start.1 = (f32[1,4,128,128]{3,2,1,0:T(8,128)S(1)}, f32[1,4,128,128]{3,2,1,0:T(8,128)S(1)}, u32[]{:S(2)}, u32[]{:S(2)}) collective-permute-start(f32[1,4,128,128]{3,2,1,0:T(8,128)S(1)} %fusion.3), channel_id=1, source_target_pairs={{4,0},{8,4},{12,8},{16,12},{20,16},{24,20},{28,24},{32,28},{36,32}... | collective-permute-start | bytes 786440 | tf_op jit(solution)/shard_map/ppermute | solution.py:13
  42.5 5.5 %collective-permute-done.1 = f32[1,4,128,128]{3,2,1,0:T(8,128)S(1)} collective-permute-done((f32[1,4,128,128]{3,2,1,0:T(8,128)S(1)}, f32[1,4,128,128]{3,2,1,0:T(8,128)S(1)}, u32[]{:S(2)}, u32[]{:S(2)}) %collective-permute-start.1) | collective-permute-done | bytes 262176 | tf_op jit(solution)/shard_map/ppermute | solution.py:13
  48.1 2.0 collective-permute-start.2
  50.2 10.8 %collective-permute-done.2 = f32[1,4,128,128]{3,2,1,0:T(8,128)S(1)} collective-permute-done((f32[1,4,128,128]{3,2,1,0:T(8,128)S(1)}, f32[1,4,128,128]{3,2,1,0:T(8,128)S(1)}, u32[]{:S(2)}, u32[]{:S(2)}) %collective-permute-start.2) | collective-permute-done | bytes 262176 | tf_op jit(solution)/shard_map/ppermute | solution.py:13
  61.5 2.7 %bitcast_multiply_fusion.15 = (f32[1,2,128,128]{3,2,1,0:T(8,128)S(1)}, f32[1,2,128,128]{3,2,1,0:T(8,128)S(1)}) fusion(pred[2,128,128]{2,1,0:T(8,128)(4,1)S(1)} %get-tuple-element.718, pred[2,128,128]{2,1,0:T(8,128)(4,1)S(1)} %get-tuple-element.717, pred[2,128,128]{2,1,0:T(8,128)(4,1)S(1)} %get-tuple-element.716, ...), kind=kLoop, calls=%fused_computation.331 | loop fusion | flops 393216 | bytes 1306640 | tf_op jit(solution)/shard_map/mul | solution.py:87
  65.0 2.7 %bitcast_multiply_fusion.14 = (f32[1,2,128,128]{3,2,1,0:T(8,128)S(1)}, f32[1,2,128,128]{3,2,1,0:T(8,128)S(1)}) fusion(pred[2,128,128]{2,1,0:T(8,128)(4,1)S(1)} %get-tuple-element.718, pred[2,128,128]{2,1,0:T(8,128)(4,1)S(1)} %get-tuple-element.717, pred[2,128,128]{2,1,0:T(8,128)(4,1)S(1)} %get-tuple-element.716, ...), kind=kLoop, calls=%fused_computation.330 | loop fusion | flops 393216 | bytes 1306640 | tf_op jit(solution)/shard_map/mul | solution.py:87
  68.4 2.7 %bitcast_multiply_fusion.13 = (f32[1,2,128,128]{3,2,1,0:T(8,128)S(1)}, f32[1,2,128,128]{3,2,1,0:T(8,128)S(1)}) fusion(pred[2,128,128]{2,1,0:T(8,128)(4,1)S(1)} %get-tuple-element.718, pred[2,128,128]{2,1,0:T(8,128)(4,1)S(1)} %get-tuple-element.717, pred[2,128,128]{2,1,0:T(8,128)(4,1)S(1)} %get-tuple-element.716, ...), kind=kLoop, calls=%fused_computation.329 | loop fusion | flops 393216 | bytes 1306640 | tf_op jit(solution)/shard_map/mul | solution.py:87
  71.8 0.1 slice_multiply_fusion.181
  72.1 3.6 %collective-permute-start.3 = (f32[1,4,128,128]{3,2,1,0:T(8,128)S(1)}, f32[1,4,128,128]{3,2,1,0:T(8,128)S(1)}, u32[]{:S(2)}, u32[]{:S(2)}) collective-permute-start(f32[1,4,128,128]{3,2,1,0:T(8,128)S(1)} %pad_maximum_fusion), channel_id=1, source_target_pairs={{4,0},{8,4},{12,8},{16,12},{20,16},{24,20},{28,24},{32,28},{36,32}... | collective-permute-start | bytes 786440 | tf_op jit(solution)/shard_map/ppermute | solution.py:13
  75.7 4.9 %collective-permute-done.3 = f32[1,4,128,128]{3,2,1,0:T(8,128)S(1)} collective-permute-done((f32[1,4,128,128]{3,2,1,0:T(8,128)S(1)}, f32[1,4,128,128]{3,2,1,0:T(8,128)S(1)}, u32[]{:S(2)}, u32[]{:S(2)}) %collective-permute-start.3) | collective-permute-done | bytes 262176 | tf_op jit(solution)/shard_map/ppermute | solution.py:13
  80.6 2.1 collective-permute-start.4
  82.7 9.7 %collective-permute-done.4 = f32[1,4,128,128]{3,2,1,0:T(8,128)S(1)} collective-permute-done((f32[1,4,128,128]{3,2,1,0:T(8,128)S(1)}, f32[1,4,128,128]{3,2,1,0:T(8,128)S(1)}, u32[]{:S(2)}, u32[]{:S(2)}) %collective-permute-start.4) | collective-permute-done | bytes 262176 | tf_op jit(solution)/shard_map/ppermute | solution.py:13
  92.5 1.9 collective-permute-start.5
  94.4 9.3 %collective-permute-done.5 = f32[1,4,128,128]{3,2,1,0:T(8,128)S(1)} collective-permute-done((f32[1,4,128,128]{3,2,1,0:T(8,128)S(1)}, f32[1,4,128,128]{3,2,1,0:T(8,128)S(1)}, u32[]{:S(2)}, u32[]{:S(2)}) %collective-permute-start.5) | collective-permute-done | bytes 262176 | tf_op jit(solution)/shard_map/ppermute | solution.py:13
  104.4 2.7 %bitcast_multiply_fusion.12 = (f32[1,2,128,128]{3,2,1,0:T(8,128)S(1)}, f32[1,2,128,128]{3,2,1,0:T(8,128)S(1)}) fusion(pred[2,128,128]{2,1,0:T(8,128)(4,1)S(1)} %get-tuple-element.718, pred[2,128,128]{2,1,0:T(8,128)(4,1)S(1)} %get-tuple-element.717, pred[2,128,128]{2,1,0:T(8,128)(4,1)S(1)} %get-tuple-element.716, ...), kind=kLoop, calls=%fused_computation.328 | loop fusion | flops 393216 | bytes 1306640 | tf_op jit(solution)/shard_map/mul | solution.py:72
  107.8 2.7 %bitcast_multiply_fusion.11 = (f32[1,2,128,128]{3,2,1,0:T(8,128)S(1)}, f32[1,2,128,128]{3,2,1,0:T(8,128)S(1)}) fusion(pred[2,128,128]{2,1,0:T(8,128)(4,1)S(1)} %get-tuple-element.718, pred[2,128,128]{2,1,0:T(8,128)(4,1)S(1)} %get-tuple-element.717, pred[2,128,128]{2,1,0:T(8,128)(4,1)S(1)} %get-tuple-element.716, ...), kind=kLoop, calls=%fused_computation.327 | loop fusion | flops 393216 | bytes 1306640 | tf_op jit(solution)/shard_map/mul | solution.py:72
  111.3 2.7 %bitcast_multiply_fusion.10 = (f32[1,2,128,128]{3,2,1,0:T(8,128)S(1)}, f32[1,2,128,128]{3,2,1,0:T(8,128)S(1)}) fusion(pred[2,128,128]{2,1,0:T(8,128)(4,1)S(1)} %get-tuple-element.718, pred[2,128,128]{2,1,0:T(8,128)(4,1)S(1)} %get-tuple-element.717, pred[2,128,128]{2,1,0:T(8,128)(4,1)S(1)} %get-tuple-element.716, ...), kind=kLoop, calls=%fused_computation.326 | loop fusion | flops 393216 | bytes 1306640 | tf_op jit(solution)/shard_map/mul | solution.py:72
  114.7 2.7 %bitcast_multiply_fusion.9 = (f32[1,2,128,128]{3,2,1,0:T(8,128)S(1)}, f32[1,2,128,128]{3,2,1,0:T(8,128)S(1)}) fusion(pred[2,128,128]{2,1,0:T(8,128)(4,1)S(1)} %get-tuple-element.718, pred[2,128,128]{2,1,0:T(8,128)(4,1)S(1)} %get-tuple-element.717, pred[2,128,128]{2,1,0:T(8,128)(4,1)S(1)} %get-tuple-element.716, ...), kind=kLoop, calls=%fused_computation.325 | loop fusion | flops 393216 | bytes 1306640 | tf_op jit(solution)/shard_map/mul | solution.py:72
  117.5 2.8 %collective-permute-start.6 = (f32[1,4,128,128]{3,2,1,0:T(8,128)S(1)}, f32[1,4,128,128]{3,2,1,0:T(8,128)S(1)}, u32[]{:S(2)}, u32[]{:S(2)}) collective-permute-start(f32[1,4,128,128]{3,2,1,0:T(8,128)S(1)} %fusion.10), channel_id=1, source_target_pairs={{4,0},{8,4},{12,8},{16,12},{20,16},{24,20},{28,24},{32,28},{36,32}... | collective-permute-start | bytes 786440 | tf_op jit(solution)/shard_map/ppermute | solution.py:13
  120.3 8.3 %collective-permute-done.6 = f32[1,4,128,128]{3,2,1,0:T(8,128)S(1)} collective-permute-done((f32[1,4,128,128]{3,2,1,0:T(8,128)S(1)}, f32[1,4,128,128]{3,2,1,0:T(8,128)S(1)}, u32[]{:S(2)}, u32[]{:S(2)}) %collective-permute-start.6) | collective-permute-done | bytes 262176 | tf_op jit(solution)/shard_map/ppermute | solution.py:13
  128.6 2.1 collective-permute-start.7
  130.7 9.2 %collective-permute-done.7 = f32[1,4,128,128]{3,2,1,0:T(8,128)S(1)} collective-permute-done((f32[1,4,128,128]{3,2,1,0:T(8,128)S(1)}, f32[1,4,128,128]{3,2,1,0:T(8,128)S(1)}, u32[]{:S(2)}, u32[]{:S(2)}) %collective-permute-start.7) | collective-permute-done | bytes 262176 | tf_op jit(solution)/shard_map/ppermute | solution.py:13
  140.4 2.7 %bitcast_multiply_fusion.8 = (f32[1,2,128,128]{3,2,1,0:T(8,128)S(1)}, f32[1,2,128,128]{3,2,1,0:T(8,128)S(1)}) fusion(pred[2,128,128]{2,1,0:T(8,128)(4,1)S(1)} %get-tuple-element.718, pred[2,128,128]{2,1,0:T(8,128)(4,1)S(1)} %get-tuple-element.717, pred[2,128,128]{2,1,0:T(8,128)(4,1)S(1)} %get-tuple-element.716, ...), kind=kLoop, calls=%fused_computation.324 | loop fusion | flops 393216 | bytes 1306640 | tf_op jit(solution)/shard_map/mul | solution.py:87
  143.6 0.1 add_divide_fusion.31
  143.8 2.7 %bitcast_multiply_fusion.7 = (f32[1,2,128,128]{3,2,1,0:T(8,128)S(1)}, f32[1,2,128,128]{3,2,1,0:T(8,128)S(1)}) fusion(pred[2,128,128]{2,1,0:T(8,128)(4,1)S(1)} %get-tuple-element.718, pred[2,128,128]{2,1,0:T(8,128)(4,1)S(1)} %get-tuple-element.717, pred[2,128,128]{2,1,0:T(8,128)(4,1)S(1)} %get-tuple-element.716, ...), kind=kLoop, calls=%fused_computation.323 | loop fusion | flops 393216 | bytes 1306640 | tf_op jit(solution)/shard_map/mul | solution.py:87
  147.3 2.7 %bitcast_multiply_fusion.6 = (f32[1,2,128,128]{3,2,1,0:T(8,128)S(1)}, f32[1,2,128,128]{3,2,1,0:T(8,128)S(1)}) fusion(pred[2,128,128]{2,1,0:T(8,128)(4,1)S(1)} %get-tuple-element.718, pred[2,128,128]{2,1,0:T(8,128)(4,1)S(1)} %get-tuple-element.717, pred[2,128,128]{2,1,0:T(8,128)(4,1)S(1)} %get-tuple-element.716, ...), kind=kLoop, calls=%fused_computation.322 | loop fusion | flops 393216 | bytes 1306640 | tf_op jit(solution)/shard_map/mul | solution.py:87
  150.6 0.1 slice_multiply_fusion.89
  150.9 1.9 collective-permute-start.8
  152.9 6.3 %collective-permute-done.8 = f32[1,4,128,128]{3,2,1,0:T(8,128)S(1)} collective-permute-done((f32[1,4,128,128]{3,2,1,0:T(8,128)S(1)}, f32[1,4,128,128]{3,2,1,0:T(8,128)S(1)}, u32[]{:S(2)}, u32[]{:S(2)}) %collective-permute-start.8) | collective-permute-done | bytes 262176 | tf_op jit(solution)/shard_map/ppermute | solution.py:13
  159.3 1.9 collective-permute-start.9
  161.2 7.3 %collective-permute-done.9 = f32[1,4,128,128]{3,2,1,0:T(8,128)S(1)} collective-permute-done((f32[1,4,128,128]{3,2,1,0:T(8,128)S(1)}, f32[1,4,128,128]{3,2,1,0:T(8,128)S(1)}, u32[]{:S(2)}, u32[]{:S(2)}) %collective-permute-start.9) | collective-permute-done | bytes 262176 | tf_op jit(solution)/shard_map/ppermute | solution.py:13
  168.5 2.9 %collective-permute-start.10 = (f32[1,4,128,128]{3,2,1,0:T(8,128)S(1)}, f32[1,4,128,128]{3,2,1,0:T(8,128)S(1)}, u32[]{:S(2)}, u32[]{:S(2)}) collective-permute-start(f32[1,4,128,128]{3,2,1,0:T(8,128)S(1)} %bitcast_select_fusion), channel_id=1, source_target_pairs={{0,4},{4,8},{8,12},{12,16},{16,20},{20,24},{24,28},{28,32},{32,36}... | collective-permute-start | bytes 786440 | tf_op jit(solution)/shard_map/ppermute | solution.py:13
  171.4 8.4 %collective-permute-done.10 = f32[1,4,128,128]{3,2,1,0:T(8,128)S(1)} collective-permute-done((f32[1,4,128,128]{3,2,1,0:T(8,128)S(1)}, f32[1,4,128,128]{3,2,1,0:T(8,128)S(1)}, u32[]{:S(2)}, u32[]{:S(2)}) %collective-permute-start.10) | collective-permute-done | bytes 262176 | tf_op jit(solution)/shard_map/ppermute | solution.py:13
  180.4 2.7 %bitcast_multiply_fusion.5 = (f32[1,2,128,128]{3,2,1,0:T(8,128)S(1)}, f32[1,2,128,128]{3,2,1,0:T(8,128)S(1)}) fusion(pred[2,128,128]{2,1,0:T(8,128)(4,1)S(1)} %get-tuple-element.718, pred[2,128,128]{2,1,0:T(8,128)(4,1)S(1)} %get-tuple-element.717, pred[2,128,128]{2,1,0:T(8,128)(4,1)S(1)} %get-tuple-element.716, ...), kind=kLoop, calls=%fused_computation.321 | loop fusion | flops 393216 | bytes 1306640 | tf_op jit(solution)/shard_map/mul | solution.py:72
  183.8 2.7 %bitcast_multiply_fusion.4 = (f32[1,2,128,128]{3,2,1,0:T(8,128)S(1)}, f32[1,2,128,128]{3,2,1,0:T(8,128)S(1)}) fusion(pred[2,128,128]{2,1,0:T(8,128)(4,1)S(1)} %get-tuple-element.718, pred[2,128,128]{2,1,0:T(8,128)(4,1)S(1)} %get-tuple-element.717, pred[2,128,128]{2,1,0:T(8,128)(4,1)S(1)} %get-tuple-element.716, ...), kind=kLoop, calls=%fused_computation.320 | loop fusion | flops 393216 | bytes 1306640 | tf_op jit(solution)/shard_map/mul | solution.py:72
  187.0 0.1 add_divide_fusion.16
  187.3 2.7 %bitcast_multiply_fusion.3 = (f32[1,2,128,128]{3,2,1,0:T(8,128)S(1)}, f32[1,2,128,128]{3,2,1,0:T(8,128)S(1)}) fusion(pred[2,128,128]{2,1,0:T(8,128)(4,1)S(1)} %get-tuple-element.718, pred[2,128,128]{2,1,0:T(8,128)(4,1)S(1)} %get-tuple-element.717, pred[2,128,128]{2,1,0:T(8,128)(4,1)S(1)} %get-tuple-element.716, ...), kind=kLoop, calls=%fused_computation.319 | loop fusion | flops 393216 | bytes 1306640 | tf_op jit(solution)/shard_map/mul | solution.py:72
  190.9 0.6 copy-done.3
  191.6 1.9 collective-permute-start.11
  193.5 9.1 %collective-permute-done.11 = f32[1,4,128,128]{3,2,1,0:T(8,128)S(1)} collective-permute-done((f32[1,4,128,128]{3,2,1,0:T(8,128)S(1)}, f32[1,4,128,128]{3,2,1,0:T(8,128)S(1)}, u32[]{:S(2)}, u32[]{:S(2)}) %collective-permute-start.11) | collective-permute-done | bytes 262176 | tf_op jit(solution)/shard_map/ppermute | solution.py:13
  202.7 1.9 collective-permute-start.12
  204.6 9.4 %collective-permute-done.12 = f32[1,4,128,128]{3,2,1,0:T(8,128)S(1)} collective-permute-done((f32[1,4,128,128]{3,2,1,0:T(8,128)S(1)}, f32[1,4,128,128]{3,2,1,0:T(8,128)S(1)}, u32[]{:S(2)}, u32[]{:S(2)}) %collective-permute-start.12) | collective-permute-done | bytes 262176 | tf_op jit(solution)/shard_map/ppermute | solution.py:13
  214.5 2.7 %bitcast_multiply_fusion.2 = (f32[1,2,128,128]{3,2,1,0:T(8,128)S(1)}, f32[1,2,128,128]{3,2,1,0:T(8,128)S(1)}) fusion(pred[2,128,128]{2,1,0:T(8,128)(4,1)S(1)} %get-tuple-element.718, pred[2,128,128]{2,1,0:T(8,128)(4,1)S(1)} %get-tuple-element.717, pred[2,128,128]{2,1,0:T(8,128)(4,1)S(1)} %get-tuple-element.716, ...), kind=kLoop, calls=%fused_computation.318 | loop fusion | flops 393216 | bytes 1306640 | tf_op jit(solution)/shard_map/mul | solution.py:87
  217.9 2.7 %bitcast_multiply_fusion.1 = (f32[1,2,128,128]{3,2,1,0:T(8,128)S(1)}, f32[1,2,128,128]{3,2,1,0:T(8,128)S(1)}) fusion(pred[2,128,128]{2,1,0:T(8,128)(4,1)S(1)} %get-tuple-element.718, pred[2,128,128]{2,1,0:T(8,128)(4,1)S(1)} %get-tuple-element.717, pred[2,128,128]{2,1,0:T(8,128)(4,1)S(1)} %get-tuple-element.716, ...), kind=kLoop, calls=%fused_computation.317 | loop fusion | flops 393216 | bytes 1306640 | tf_op jit(solution)/shard_map/mul | solution.py:87
  221.4 2.7 %bitcast_multiply_fusion = (f32[1,2,128,128]{3,2,1,0:T(8,128)S(1)}, f32[1,2,128,128]{3,2,1,0:T(8,128)S(1)}) fusion(pred[2,128,128]{2,1,0:T(8,128)(4,1)S(1)} %get-tuple-element.718, pred[2,128,128]{2,1,0:T(8,128)(4,1)S(1)} %get-tuple-element.717, pred[2,128,128]{2,1,0:T(8,128)(4,1)S(1)} %get-tuple-element.716, ...), kind=kLoop, calls=%fused_computation.316 | loop fusion | flops 393216 | bytes 1306640 | tf_op jit(solution)/shard_map/mul | solution.py:87
  225.0 1.9 collective-permute-start.13
  226.9 6.3 %collective-permute-done.13 = f32[1,4,128,128]{3,2,1,0:T(8,128)S(1)} collective-permute-done((f32[1,4,128,128]{3,2,1,0:T(8,128)S(1)}, f32[1,4,128,128]{3,2,1,0:T(8,128)S(1)}, u32[]{:S(2)}, u32[]{:S(2)}) %collective-permute-start.13) | collective-permute-done | bytes 262176 | tf_op jit(solution)/shard_map/ppermute | solution.py:13
  233.2 0.8 fusion.21
  (340 shorter events, 16.9 us)
Async XLA Ops:
  0.6 4.2 %copy-start.5 = (f32[4]{0:T(128)S(1)}, f32[4]{0:T(128)}, u32[]{:S(2)}) copy-start(f32[4]{0:T(128)} %param.122) | copy-start | bytes 52
  0.7 4.8 %copy-start.6 = (f32[4]{0:T(128)S(1)}, f32[4]{0:T(128)}, u32[]{:S(2)}) copy-start(f32[4]{0:T(128)} %param.123) | copy-start | bytes 52
  0.7 5.4 %copy-start.4 = (s32[2,128,128]{2,1,0:T(8,128)S(1)}, s32[2,128,128]{2,1,0:T(8,128)}, u32[]{:S(2)}) copy-start(s32[2,128,128]{2,1,0:T(8,128)} %param.119) | copy-start | bytes 393220
  1.7 17.2 %collective-permute-start = (f32[1,4,128,128]{3,2,1,0:T(8,128)S(1)}, f32[1,4,128,128]{3,2,1,0:T(8,128)S(1)}, u32[]{:S(2)}, u32[]{:S(2)}) collective-permute-start(f32[1,4,128,128]{3,2,1,0:T(8,128)S(1)} %multiply_bitcast_fusion), channel_id=1, source_target_pairs={{0,4},{4,8},{8,12},{12,16},{16,20},{20,24},{24,28},{28,32},{32,36}... | collective-permute-start | bytes 786440 | tf_op jit(solution)/shard_map/ppermute | solution.py:13
  14.2 0.9 copy-start
  35.2 12.8 %copy-start.1 = (f32[1,1,4,128,128]{4,3,2,1,0:T(8,128)S(1)}, f32[1,1,4,128,128]{4,3,2,1,0:T(8,128)}, u32[]{:S(2)}) copy-start(f32[1,1,4,128,128]{4,3,2,1,0:T(8,128)} %param.120) | copy-start | bytes 786436
  35.2 12.8 %collective-permute-start.1 = (f32[1,4,128,128]{3,2,1,0:T(8,128)S(1)}, f32[1,4,128,128]{3,2,1,0:T(8,128)S(1)}, u32[]{:S(2)}, u32[]{:S(2)}) collective-permute-start(f32[1,4,128,128]{3,2,1,0:T(8,128)S(1)} %fusion.3), channel_id=1, source_target_pairs={{4,0},{8,4},{12,8},{16,12},{20,16},{24,20},{28,24},{32,28},{36,32}... | collective-permute-start | bytes 786440 | tf_op jit(solution)/shard_map/ppermute | solution.py:13
  48.1 12.8 %collective-permute-start.2 = (f32[1,4,128,128]{3,2,1,0:T(8,128)S(1)}, f32[1,4,128,128]{3,2,1,0:T(8,128)S(1)}, u32[]{:S(2)}, u32[]{:S(2)}) collective-permute-start(f32[1,4,128,128]{3,2,1,0:T(8,128)S(1)} %fusion.2), channel_id=1, source_target_pairs={{0,4},{4,8},{8,12},{12,16},{16,20},{20,24},{24,28},{28,32},{32,36}... | collective-permute-start | bytes 786440 | tf_op jit(solution)/shard_map/ppermute | solution.py:13
  72.1 8.5 %collective-permute-start.3 = (f32[1,4,128,128]{3,2,1,0:T(8,128)S(1)}, f32[1,4,128,128]{3,2,1,0:T(8,128)S(1)}, u32[]{:S(2)}, u32[]{:S(2)}) collective-permute-start(f32[1,4,128,128]{3,2,1,0:T(8,128)S(1)} %pad_maximum_fusion), channel_id=1, source_target_pairs={{4,0},{8,4},{12,8},{16,12},{20,16},{24,20},{28,24},{32,28},{36,32}... | collective-permute-start | bytes 786440 | tf_op jit(solution)/shard_map/ppermute | solution.py:13
  80.6 11.9 %copy-start.2 = (f32[2,1,4,128,128]{4,3,2,1,0:T(8,128)S(1)}, f32[2,1,4,128,128]{4,3,2,1,0:T(8,128)}, u32[]{:S(2)}) copy-start(f32[2,1,4,128,128]{4,3,2,1,0:T(8,128)} %param.121) | copy-start | bytes 1572868
  80.6 11.8 %collective-permute-start.4 = (f32[1,4,128,128]{3,2,1,0:T(8,128)S(1)}, f32[1,4,128,128]{3,2,1,0:T(8,128)S(1)}, u32[]{:S(2)}, u32[]{:S(2)}) collective-permute-start(f32[1,4,128,128]{3,2,1,0:T(8,128)S(1)} %fusion.6), channel_id=1, source_target_pairs={{0,1},{1,2},{2,3},{4,5},{5,6},{6,7},{8,9},{9,10},{10,11},{12,13},{... | collective-permute-start | bytes 786440 | tf_op jit(solution)/shard_map/ppermute | solution.py:13
  92.5 11.3 %collective-permute-start.5 = (f32[1,4,128,128]{3,2,1,0:T(8,128)S(1)}, f32[1,4,128,128]{3,2,1,0:T(8,128)S(1)}, u32[]{:S(2)}, u32[]{:S(2)}) collective-permute-start(f32[1,4,128,128]{3,2,1,0:T(8,128)S(1)} %bitcast_select_fusion.1), channel_id=1, source_target_pairs={{0,4},{4,8},{8,12},{12,16},{16,20},{20,24},{24,28},{28,32},{32,36}... | collective-permute-start | bytes 786440 | tf_op jit(solution)/shard_map/ppermute | solution.py:13
  117.5 11.1 %collective-permute-start.6 = (f32[1,4,128,128]{3,2,1,0:T(8,128)S(1)}, f32[1,4,128,128]{3,2,1,0:T(8,128)S(1)}, u32[]{:S(2)}, u32[]{:S(2)}) collective-permute-start(f32[1,4,128,128]{3,2,1,0:T(8,128)S(1)} %fusion.10), channel_id=1, source_target_pairs={{4,0},{8,4},{12,8},{16,12},{20,16},{24,20},{28,24},{32,28},{36,32}... | collective-permute-start | bytes 786440 | tf_op jit(solution)/shard_map/ppermute | solution.py:13
  128.6 11.3 %collective-permute-start.7 = (f32[1,4,128,128]{3,2,1,0:T(8,128)S(1)}, f32[1,4,128,128]{3,2,1,0:T(8,128)S(1)}, u32[]{:S(2)}, u32[]{:S(2)}) collective-permute-start(f32[1,4,128,128]{3,2,1,0:T(8,128)S(1)} %fusion.9), channel_id=1, source_target_pairs={{0,4},{4,8},{8,12},{12,16},{16,20},{20,24},{24,28},{28,32},{32,36}... | collective-permute-start | bytes 786440 | tf_op jit(solution)/shard_map/ppermute | solution.py:13
  150.9 8.3 %collective-permute-start.8 = (f32[1,4,128,128]{3,2,1,0:T(8,128)S(1)}, f32[1,4,128,128]{3,2,1,0:T(8,128)S(1)}, u32[]{:S(2)}, u32[]{:S(2)}) collective-permute-start(f32[1,4,128,128]{3,2,1,0:T(8,128)S(1)} %pad_maximum_fusion.1), channel_id=1, source_target_pairs={{4,0},{8,4},{12,8},{16,12},{20,16},{24,20},{28,24},{32,28},{36,32}... | collective-permute-start | bytes 786440 | tf_op jit(solution)/shard_map/ppermute | solution.py:13
  159.3 9.2 %collective-permute-start.9 = (f32[1,4,128,128]{3,2,1,0:T(8,128)S(1)}, f32[1,4,128,128]{3,2,1,0:T(8,128)S(1)}, u32[]{:S(2)}, u32[]{:S(2)}) collective-permute-start(f32[1,4,128,128]{3,2,1,0:T(8,128)S(1)} %fusion.13), channel_id=1, source_target_pairs={{0,1},{1,2},{2,3},{4,5},{5,6},{6,7},{8,9},{9,10},{10,11},{12,13},{... | collective-permute-start | bytes 786440 | tf_op jit(solution)/shard_map/ppermute | solution.py:13
  168.5 11.3 %collective-permute-start.10 = (f32[1,4,128,128]{3,2,1,0:T(8,128)S(1)}, f32[1,4,128,128]{3,2,1,0:T(8,128)S(1)}, u32[]{:S(2)}, u32[]{:S(2)}) collective-permute-start(f32[1,4,128,128]{3,2,1,0:T(8,128)S(1)} %bitcast_select_fusion), channel_id=1, source_target_pairs={{0,4},{4,8},{8,12},{12,16},{16,20},{20,24},{24,28},{28,32},{32,36}... | collective-permute-start | bytes 786440 | tf_op jit(solution)/shard_map/ppermute | solution.py:13
  190.9 0.7 copy-start.3
  191.6 11.1 %collective-permute-start.11 = (f32[1,4,128,128]{3,2,1,0:T(8,128)S(1)}, f32[1,4,128,128]{3,2,1,0:T(8,128)S(1)}, u32[]{:S(2)}, u32[]{:S(2)}) collective-permute-start(f32[1,4,128,128]{3,2,1,0:T(8,128)S(1)} %fusion.17), channel_id=1, source_target_pairs={{4,0},{8,4},{12,8},{16,12},{20,16},{24,20},{28,24},{32,28},{36,32}... | collective-permute-start | bytes 786440 | tf_op jit(solution)/shard_map/ppermute | solution.py:13
  202.7 11.3 %collective-permute-start.12 = (f32[1,4,128,128]{3,2,1,0:T(8,128)S(1)}, f32[1,4,128,128]{3,2,1,0:T(8,128)S(1)}, u32[]{:S(2)}, u32[]{:S(2)}) collective-permute-start(f32[1,4,128,128]{3,2,1,0:T(8,128)S(1)} %fusion.16), channel_id=1, source_target_pairs={{0,4},{4,8},{8,12},{12,16},{16,20},{20,24},{24,28},{28,32},{32,36}... | collective-permute-start | bytes 786440 | tf_op jit(solution)/shard_map/ppermute | solution.py:13
  225.0 8.3 %collective-permute-start.13 = (f32[1,4,128,128]{3,2,1,0:T(8,128)S(1)}, f32[1,4,128,128]{3,2,1,0:T(8,128)S(1)}, u32[]{:S(2)}, u32[]{:S(2)}) collective-permute-start(f32[1,4,128,128]{3,2,1,0:T(8,128)S(1)} %pad_maximum_fusion.2), channel_id=1, source_target_pairs={{4,0},{8,4},{12,8},{16,12},{20,16},{24,20},{28,24},{32,28},{36,32}... | collective-permute-start | bytes 786440 | tf_op jit(solution)/shard_map/ppermute | solution.py:13
where the time goes:
time: 235 us; the launch traced here: 234 us
  waiting for transfers between devices  105 us (45%)
  other arithmetic  85.5 us (36%)
  starting transfers between devices  37.3 us (16%)
  local copies, waits for them, and re-layouts  3.7 us (2%)
  between operations  2.94 us (1%)
    ppermute x14, waiting for transfers between devices, shifted(): lax.ppermute(value, axis, [(source, source + steps) for source in range(l...  105 us
    ppermute x14, starting transfers between devices, shifted(): lax.ppermute(value, axis, [(source, source + steps) for source in range(l...  37.3 us
    mul x11, other arithmetic, neumann(): rhs = capacity * psi  31.7 us
    mul x11, other arithmetic, dirichlet(): rhs = capacity * state  29.4 us
    div x52, other arithmetic, relax(): value = (rhs + near) / diag  8.49 us
    mul x68, other arithmetic, relax(): face_z * value[:, :, :, :-1]  6.79 us
  transfers between devices with their start and end apart: 14, of which 13 were waited for; matrix products, arithmetic and copies ran while one was open for 6% of the time, Pallas kernels for 0%

commit v1 on v0

v1 whole, which is shorter than its diff:
```python
import functools

import jax
import jax.numpy as jnp
from jax import lax
from jax.experimental import pallas as pl
from jax.experimental.pallas import tpu as pltpu
from jax.sharding import PartitionSpec as P

MESH = pl.DeviceIdType.MESH
TICKS = 3
STEPS = 4
NY = 128
NZ = 128
PAD = 8
ROWS = NY + 2 * PAD
CHUNK = 32
F32 = jnp.float32


def harmonic(first, second):
    return 2.0 * first * second / (first + second)


def sweep(source, target, rhs, coeff, extra=None):
    for plane in range(2):
        for row in range(0, NY, CHUNK):
            here = slice(row, row + CHUNK)
            base = PAD + row
            v = source[plane, base : base + CHUNK, :]
            out = rhs[plane, here, :]
            out = out + coeff[0, plane, here, :] * source[1 - plane, base : base + CHUNK, :]
            out = out + coeff[1, plane, here, :] * source[plane, base - 1 : base - 1 + CHUNK, :]
            out = out + coeff[2, plane, here, :] * source[plane, base + 1 : base + 1 + CHUNK, :]
            out = out + coeff[3, plane, here, :] * pltpu.roll(v, 1, 1)
            out = out + coeff[4, plane, here, :] * pltpu.roll(v, NZ - 1, 1)
            target[plane, base : base + CHUNK, :] = out
            if extra is not None:
                extra(plane, here, out)


def kernel(
    cond_ref, cap_ref, fields, labels, traces, guess,
    out_u, out_h,
    stage_lab, stage_u, stage_h, lab, u, h_right, h_left, guess_right, guess_left,
    psi, buf_a, buf_b, rhs, co_d, co_n, end, inv_n,
    qf, ql, q_left, q_right, pf, plast, p_left, p_right, back,
    lab_sem, u_sem, h_sem, hl_sem, gr_sem, gl_sem,
    q_sem, p_sem, out_sem, load_sem, send_sem, qs_sem, ps_sem, hs_sem, bs_sem,
):
    sub = lax.axis_index("sub")
    it = lax.axis_index("iter")
    pair = sub // 2
    xl = sub % 2
    xh = it // 2
    core = it % 2
    ring = 2 * xh + xl
    slab = 2 * pair + core
    pairs = lax.axis_size("sub") // 2
    has_left = slab > 0
    has_right = slab < 2 * pairs - 1
    swapped = xl != core
    stays = xl == core
    takes_guess = xh == 1

    right_id = {"sub": sub + 2 * core, "iter": it + 1 - 2 * core}
    left_id = {"sub": sub - 2 * (1 - core), "iter": it + 1 - 2 * core}
    partner_id = {"sub": sub + 1 - 2 * xl, "iter": it + 1 - 2 * core}
    down = (ring + 3) % 4
    up = (ring + 1) % 4
    down_id = {"sub": 2 * pair + down % 2, "iter": 2 * (down // 2) + core}
    up_id = {"sub": 2 * pair + up % 2, "iter": 2 * (up // 2) + core}
    home_id = {"sub": 2 * pair + core, "iter": (ring + 2) % 4}
    source_ring = (it + 2) % 4
    source_id = {"sub": 2 * pair + source_ring % 2, "iter": 2 * (source_ring // 2) + xl}

    def remote(src, dst, send, recv, device):
        return pltpu.make_async_remote_copy(
            src_ref=src, dst_ref=dst, send_sem=send, recv_sem=recv, device_id=device, device_id_type=MESH
        )

    inner = pl.ds(PAD, NY)

    zero_pad = jnp.zeros((2, PAD, NZ), F32)
    for ref in (buf_a, buf_b, psi):
        ref[:, 0:PAD, :] = zero_pad
        ref[:, PAD + NY : ROWS, :] = zero_pad
    for tick in range(TICKS):
        u[tick, :, 0:PAD, :] = zero_pad
        u[tick, :, PAD + NY : ROWS, :] = zero_pad

    barrier = pltpu.get_barrier_semaphore()

    def greet(device):
        pl.semaphore_signal(barrier, inc=1, device_id=device, device_id_type=MESH)

    pl.when(has_left)(lambda: greet(left_id))
    pl.when(has_right)(lambda: greet(right_id))
    pl.when(swapped)(lambda: greet(partner_id))
    greet(up_id)
    greet(source_id)

    def loads(d_h, d_lab, d_u):
        return [
            pltpu.make_async_copy(traces.at[0, 0], d_h, load_sem.at[0]),
            pltpu.make_async_copy(labels, d_lab, load_sem.at[1]),
            pltpu.make_async_copy(fields.at[0], d_u, load_sem.at[2]),
        ]

    keep = loads(h_right, lab, u.at[0, :, inner, :])
    pass_on = loads(stage_h, stage_lab, stage_u)
    keep_guess = pltpu.make_async_copy(guess.at[1 - xl, 0], guess_right, gr_sem)

    @pl.when(stays)
    def _():
        for copy in keep:
            copy.start()

    @pl.when(swapped)
    def _():
        for copy in pass_on:
            copy.start()

    @pl.when(jnp.logical_and(stays, takes_guess))
    def _():
        keep_guess.start()

    peers = 2 + (xl + core) % 2 + jnp.where(has_left, 1, 0) + jnp.where(has_right, 1, 0)
    pl.semaphore_wait(barrier, peers)

    swap_h = [
        remote(stage_h.at[n], h_right.at[n], send_sem.at[n], h_sem.at[n], partner_id) for n in range(STEPS)
    ]
    swap_lab = remote(stage_lab, lab, send_sem.at[4], lab_sem, partner_id)
    swap_u = remote(stage_u, u.at[0, :, inner, :], send_sem.at[5], u_sem.at[0], partner_id)
    swap_guess = remote(guess.at[xl, 0], guess_right, send_sem.at[6], gr_sem, partner_id)
    pass_guess = remote(guess_right, guess_left, send_sem.at[7], gl_sem, right_id)
    move_u = [
        remote(u.at[t, :, inner, :], u.at[t + 1, :, inner, :], send_sem.at[8 + t], u_sem.at[t + 1], down_id)
        for t in range(TICKS - 1)
    ]
    home_u = remote(u.at[TICKS - 1, :, inner, :], out_u.at[0], send_sem.at[8 + TICKS], out_sem.at[STEPS], home_id)

    def pass_h(n):
        return remote(h_right.at[n], h_left.at[n], hs_sem.at[n], hl_sem.at[n], right_id)

    def send_qf(t, n):
        return remote(qf.at[t, n], q_right.at[t, n], qs_sem.at[t, 0, n], q_sem.at[t, 1, n], left_id)

    def send_ql(t, n):
        return remote(ql.at[t, n], q_left.at[t, n], qs_sem.at[t, 1, n], q_sem.at[t, 0, n], right_id)

    def send_pf(t, n):
        return remote(pf.at[t, n], p_right.at[t, n], ps_sem.at[t, 0, n], p_sem.at[t, 1, n], left_id)

    def send_pl(t, n):
        return remote(plast.at[t, n], p_left.at[t, n], ps_sem.at[t, 1, n], p_sem.at[t, 0, n], right_id)

    def send_home(n):
        return remote(back.at[n], out_h.at[0, 0, n], bs_sem.at[n], out_sem.at[n], home_id)

    @pl.when(swapped)
    def _():
        pass_on[0].wait()
        for copy in swap_h:
            copy.start()
        pass_on[1].wait()
        swap_lab.start()
        pass_on[2].wait()
        swap_u.start()

    @pl.when(jnp.logical_and(swapped, takes_guess))
    def _():
        swap_guess.start()

    @pl.when(stays)
    def _():
        keep[0].wait()

    for n in range(STEPS):
        pl.when(swapped)(swap_h[n].wait_recv)
        pl.when(has_right)(pass_h(n).start)

    @pl.when(jnp.logical_not(has_right))
    def _():
        h_right[...] = jnp.zeros((STEPS, NY, NZ), F32)

    @pl.when(jnp.logical_not(has_left))
    def _():
        h_left[...] = jnp.zeros((STEPS, NY, NZ), F32)

    pl.when(stays)(keep[1].wait)
    pl.when(swapped)(swap_lab.wait_recv)

    def pick(table, value):
        result = jnp.full(value.shape, table[0], F32)
        for cls in range(1, 4):
            result = jnp.where(value == cls, table[cls], result)
        return result

    for plane in range(2):
        for row in range(0, NY, CHUNK):
            buf_a[plane, PAD + row : PAD + row + CHUNK, :] = pick(cond_ref, lab[plane, row : row + CHUNK, :])
    lane = lax.broadcasted_iota(jnp.int32, (CHUNK, NZ), 1)
    line = lax.broadcasted_iota(jnp.int32, (CHUNK, NZ), 0)
    for plane in range(2):
        edge = has_left if plane == 0 else has_right
        for row in range(0, NY, CHUNK):
            here = slice(row, row + CHUNK)
            base = PAD + row
            k = buf_a[plane, base : base + CHUNK, :]
            twice = 2.0 * k
            face_x = harmonic(k, buf_a[1 - plane, base : base + CHUNK, :])
            face_u = harmonic(k, buf_a[plane, base - 1 : base - 1 + CHUNK, :])
            face_d = harmonic(k, buf_a[plane, base + 1 : base + 1 + CHUNK, :])
            face_l = jnp.where(lane == 0, 0.0, harmonic(k, pltpu.roll(k, 1, 1)))
            face_r = jnp.where(lane == NZ - 1, 0.0, harmonic(k, pltpu.roll(k, NZ - 1, 1)))
            side_u = jnp.where(line + row == 0, twice, face_u) if row == 0 else face_u
            side_d = jnp.where(line + row == NY - 1, twice, face_d) if row + CHUNK == NY else face_d
            side_l = jnp.where(lane == 0, twice, face_l)
            side_r = jnp.where(lane == NZ - 1, twice, face_r)
            capacity = pick(cap_ref, lab[plane, here, :])
            common = capacity + face_x + side_u + side_d + side_l + side_r
            inv_dir = 1.0 / (common + twice)
            inv_neu = 1.0 / jnp.where(edge, common, common + twice)
            faces = (face_x, face_u, face_d, face_l, face_r, capacity)
            for j, face in enumerate(faces):
                co_d[j, plane, here, :] = face * inv_dir
                co_n[j, plane, here, :] = face * inv_neu
            co_d[6, plane, here, :] = twice * inv_dir
            end[plane, here, :] = twice
            inv_n[plane, here, :] = inv_neu

    pl.when(stays)(keep[2].wait)
    pl.when(swapped)(swap_u.wait_recv)

    for tick in range(TICKS):
        state = u.at[tick]
        if tick > 0:
            restart = ring == (4 - tick)
            restart_r = jnp.logical_and(restart, has_right)
            restart_l = jnp.logical_and(restart, has_left)
            move_u[tick - 1].wait_recv()
            if tick == 1:
                pl.when(jnp.logical_and(takes_guess, has_left))(pass_guess.wait_recv)

        def dirichlet(n, carry, tick=tick, state=state):
            if tick == 0:
                pl.when(has_left)(pass_h(n).wait_recv)
            else:
                pl.when(has_right)(send_pf(tick - 1, n).wait_recv)
                pl.when(has_left)(send_pl(tick - 1, n).wait_recv)
                if tick == 1:
                    pl.when(has_right)(pass_h(n).wait_send)
                for row in range(0, NY, CHUNK):
                    here = slice(row, row + CHUNK)
                    old = h_right[n, here, :]
                    new = old + 0.25 * (plast[tick - 1, n, here, :] + p_right[tick - 1, n, here, :])
                    new = jnp.where(has_right, new, 0.0)
                    h_right[n, here, :] = jnp.where(restart_r, guess_right[n, here, :], new)
                    old = h_left[n, here, :]
                    new = old + 0.25 * (p_left[tick - 1, n, here, :] + pf[tick - 1, n, here, :])
                    new = jnp.where(has_left, new, 0.0)
                    h_left[n, here, :] = jnp.where(restart_l, guess_left[n, here, :], new)
            for plane, trace in enumerate((h_left, h_right)):
                for row in range(0, NY, CHUNK):
                    here = slice(row, row + CHUNK)
                    rhs[plane, here, :] = (
                        co_d[5, plane, here, :] * state[plane, PAD + row : PAD + row + CHUNK, :]
                        + co_d[6, plane, here, :] * trace[n, here, :]
                    )

            def flux(plane, here, value):
                if plane == 0:
                    qf[tick, n, here, :] = end[0, here, :] * (value - h_left[n, here, :])
                else:
                    ql[tick, n, here, :] = end[1, here, :] * (value - h_right[n, here, :])

            sweep(state, buf_a, rhs, co_d)
            sweep(buf_a, buf_b, rhs, co_d)
            sweep(buf_b, state, rhs, co_d, flux)
            pl.when(has_right)(send_ql(tick, n).start)
            pl.when(has_left)(send_qf(tick, n).start)
            return carry

        lax.fori_loop(0, STEPS, dirichlet, 0)
        if tick + 1 < TICKS:
            move_u[tick].start()
        else:
            home_u.start()
        if tick == 0:

            @pl.when(takes_guess)
            def _():
                pl.when(stays)(keep_guess.wait)
                pl.when(swapped)(swap_guess.wait_recv)
                pl.when(has_right)(pass_guess.start)

        def neumann(n, carry, tick=tick, first=False):
            pl.when(has_right)(send_qf(tick, n).wait_recv)
            pl.when(has_left)(send_ql(tick, n).wait_recv)
            for plane in range(2):
                own, got, edge = ((qf, q_left, has_left), (ql, q_right, has_right))[plane]
                for row in range(0, NY, CHUNK):
                    here = slice(row, row + CHUNK)
                    jump = own[tick, n, here, :] + got[tick, n, here, :]
                    value = inv_n[plane, here, :] * jnp.where(edge, jump, 0.0)
                    if not first:
                        value = value + co_n[5, plane, here, :] * psi[plane, PAD + row : PAD + row + CHUNK, :]
                    rhs[plane, here, :] = value
                    if first:
                        buf_a[plane, PAD + row : PAD + row + CHUNK, :] = value

            def ends(plane, here, value):
                (pf, plast)[plane][tick, n, here, :] = value

            if not first:
                sweep(psi, buf_a, rhs, co_n)
            sweep(buf_a, buf_b, rhs, co_n)
            sweep(buf_b, psi, rhs, co_n, ends)
            pl.when(has_left)(send_pf(tick, n).start)
            if tick + 1 < TICKS:
                pl.when(has_right)(send_pl(tick, n).start)
            return carry

        neumann(0, 0, first=True)
        lax.fori_loop(1, STEPS, neumann, 0)

    last = TICKS - 1

    def finish(n, carry):
        pl.when(has_right)(send_pf(last, n).wait_recv)
        for row in range(0, NY, CHUNK):
            here = slice(row, row + CHUNK)
            new = h_right[n, here, :] + 0.25 * (plast[last, n, here, :] + p_right[last, n, here, :])
            back[n, here, :] = jnp.where(has_right, new, 0.0)
        send_home(n).start()
        return carry

    lax.fori_loop(0, STEPS, finish, 0)

    @pl.when(swapped)
    def _():
        for copy in swap_h:
            copy.wait_send()
        swap_lab.wait_send()
        swap_u.wait_send()

    pl.when(jnp.logical_and(swapped, takes_guess))(swap_guess.wait_send)
    pl.when(jnp.logical_and(takes_guess, has_right))(pass_guess.wait_send)
    for copy in move_u:
        copy.wait_send()
    home_u.wait_send()

    @pl.when(has_right)
    def _():
        for n in range(STEPS):
            for t in range(TICKS):
                send_ql(t, n).wait_send()
                if t < last:
                    send_pl(t, n).wait_send()

    @pl.when(has_left)
    def _():
        for n in range(STEPS):
            for t in range(TICKS):
                send_qf(t, n).wait_send()
                send_pf(t, n).wait_send()

    for n in range(STEPS):
        send_home(n).wait_send()
    home_u.wait_recv()
    for n in range(STEPS):
        send_home(n).wait_recv()


def local(fields, labels, traces, new_guess, cond_table, cap_table):
    plane = (NY, NZ)
    field = (2, ROWS, NZ)
    vm = lambda *shape: pltpu.VMEM(shape, F32)
    dma = lambda *shape: pltpu.SemaphoreType.DMA(shape)
    any_spec = pl.BlockSpec(memory_space=pl.ANY)
    smem = pl.BlockSpec(memory_space=pltpu.SMEM)
    per_step = (TICKS, STEPS) + plane
    return pl.pallas_call(
        kernel,
        out_shape=(
            jax.ShapeDtypeStruct((1, 2) + plane, F32),
            jax.ShapeDtypeStruct((1, 1, STEPS) + plane, F32),
        ),
        in_specs=[smem, smem, any_spec, any_spec, any_spec, any_spec],
        out_specs=(any_spec, any_spec),
        scratch_shapes=[
            pltpu.VMEM((2,) + plane, jnp.int32),
            vm(2, *plane),
            vm(STEPS, *plane),
            pltpu.VMEM((2,) + plane, jnp.int32),
            vm(TICKS, *field),
            vm(STEPS, *plane),
            vm(STEPS, *plane),
            vm(STEPS, *plane),
            vm(STEPS, *plane),
            vm(*field),
            vm(*field),
            vm(*field),
            vm(2, *plane),
            vm(7, 2, *plane),
            vm(6, 2, *plane),
            vm(2, *plane),
            vm(2, *plane),
            vm(*per_step),
            vm(*per_step),
            vm(*per_step),
            vm(*per_step),
            vm(*per_step),
            vm(*per_step),
            vm(*per_step),
            vm(*per_step),
            vm(STEPS, *plane),
            pltpu.SemaphoreType.DMA,
            dma(TICKS),
            dma(STEPS),
            dma(STEPS),
            pltpu.SemaphoreType.DMA,
            pltpu.SemaphoreType.DMA,
            dma(TICKS, 2, STEPS),
            dma(TICKS, 2, STEPS),
            dma(STEPS + 1),
            dma(3),
            dma(8 + TICKS + 1),
            dma(TICKS, 2, STEPS),
            dma(TICKS, 2, STEPS),
            dma(STEPS),
            dma(STEPS),
        ],
        compiler_params=pltpu.CompilerParams(collective_id=0, has_side_effects=True),
    )(cond_table, cap_table, fields, labels, traces, new_guess)


def solution(mesh):
    return jax.shard_map(
        local,
        mesh=mesh,
        in_specs=(
            P("iter", "sub", None, None),
            P("sub", None, None),
            P("iter", "sub", None, None, None),
            P(None, "sub", None, None, None),
            P(),
            P(),
        ),
        out_specs=(P("iter", "sub", None, None), P("iter", "sub", None, None, None)),
        check_vma=False,
    )
```

time: 235 us -> 50.3 us (0.21)
  the two profiles are of different devices: /device:TPU:12 before, /device:TPU:24 now
where the time goes in v1:
time: 50.3 us; the launch traced here: 50.2 us
  Pallas kernels  47.3 us (94%)
  local copies, waits for them, and re-layouts  2.32 us (5%)
  between operations  0.65 us (1%)
    pallas_call x1, Pallas kernels, local(): pl.pallas_call(kernel, out_shape=(jax.ShapeDtypeStruct((1, 2) + plane, F3...  47.3 us
    unnamed x4, local copies, waits for them, and re-layouts  2.32 us

profile of v1, /device:TPU:24, one launch (start us, length us, event | category | flops | bytes accessed | tf_op | source)
XLA Modules:
  0.0 50.2 jit_solution(8205885000136465417)
XLA Ops:
  0.6 47.3 %shard_map.77 = (f32[1,2,128,128]{3,2,1,0:T(8,128)}, f32[1,1,4,128,128]{4,3,2,1,0:T(8,128)}) custom-call(f32[4]{0:T(128)} %cond_ref.1, f32[4]{0:T(128)} %cap_ref.1, f32[1,2,128,128]{3,2,1,0:T(8,128)} %fields.1, s32[2,128,128]{2,1,0:T(8,128)} %labels.1, f32[1,1,4,128,128]{4,3,2,1,0:T(8,128)} %traces.1, f32[2,1,4,128,128]{4,3,2,1,0:T(8,128)} %guess.1), custom_call_target="tpu_custom_call" | custom-call | tf_op jit(solution)/shard_map/pallas_call | solution.py:385
  47.9 0.0 copy-start
  47.9 1.6 %copy.10 = f32[1,2,128,128]{3,2,1,0:T(8,128)} copy(f32[1,2,128,128]{3,2,1,0:T(8,128)} %get-tuple-element.4) | data formatting | bytes 262144
  49.5 0.0 copy-done
  49.5 0.7 %copy.11 = f32[1,1,4,128,128]{4,3,2,1,0:T(8,128)} copy(f32[1,1,4,128,128]{4,3,2,1,0:T(8,128)S(1)} %copy-done) | data formatting | bytes 524288
Async XLA Ops:
  47.9 1.6 %copy-start = (f32[1,1,4,128,128]{4,3,2,1,0:T(8,128)S(1)}, f32[1,1,4,128,128]{4,3,2,1,0:T(8,128)}, u32[]{:S(2)}) copy-start(f32[1,1,4,128,128]{4,3,2,1,0:T(8,128)} %get-tuple-element.5) | copy-start | bytes 786436

commit v2 on v1

--- a/solution.py
+++ b/solution.py
@@ -40,8 +40,9 @@
 
 
 def kernel(
-    cond_ref, cap_ref, fields, labels, traces, guess,
+    cond_hbm, cap_hbm, fields, labels, traces, guess,
     out_u, out_h,
+    cond_ref, cap_ref,
     stage_lab, stage_u, stage_h, lab, u, h_right, h_left, guess_right, guess_left,
     psi, buf_a, buf_b, rhs, co_d, co_n, end, inv_n,
     qf, ql, q_left, q_right, pf, plast, p_left, p_right, back,
@@ -70,6 +71,8 @@
     up = (ring + 1) % 4
     down_id = {"sub": 2 * pair + down % 2, "iter": 2 * (down // 2) + core}
     up_id = {"sub": 2 * pair + up % 2, "iter": 2 * (up // 2) + core}
+    other = (ring + 1 + 2 * core) % 4
+    other_id = {"sub": 2 * pair + other % 2, "iter": 2 * (other // 2) + 1 - core}
     home_id = {"sub": 2 * pair + core, "iter": (ring + 2) % 4}
     source_ring = (it + 2) % 4
     source_id = {"sub": 2 * pair + source_ring % 2, "iter": 2 * (source_ring // 2) + xl}
@@ -97,20 +100,29 @@
     pl.when(has_left)(lambda: greet(left_id))
     pl.when(has_right)(lambda: greet(right_id))
     pl.when(swapped)(lambda: greet(partner_id))
+    pl.when(swapped)(lambda: greet(other_id))
     greet(up_id)
     greet(source_id)
 
     def loads(d_h, d_lab, d_u):
         return [
-            pltpu.make_async_copy(traces.at[0, 0], d_h, load_sem.at[0]),
+            pltpu.make_async_copy(traces.at[0, 0, 0:1], d_h.at[0:1], load_sem.at[0]),
             pltpu.make_async_copy(labels, d_lab, load_sem.at[1]),
             pltpu.make_async_copy(fields.at[0], d_u, load_sem.at[2]),
+            pltpu.make_async_copy(traces.at[0, 0, 1:STEPS], d_h.at[1:STEPS], load_sem.at[3]),
         ]
 
     keep = loads(h_right, lab, u.at[0, :, inner, :])
     pass_on = loads(stage_h, stage_lab, stage_u)
     keep_guess = pltpu.make_async_copy(guess.at[1 - xl, 0], guess_right, gr_sem)
 
+    tables = [
+        pltpu.make_async_copy(cond_hbm, cond_ref, load_sem.at[4]),
+        pltpu.make_async_copy(cap_hbm, cap_ref, load_sem.at[5]),
+    ]
+    for copy in tables:
+        copy.start()
+
     @pl.when(stays)
     def _():
         for copy in keep:
@@ -125,13 +137,13 @@
     def _():
         keep_guess.start()
 
-    peers = 2 + (xl + core) % 2 + jnp.where(has_left, 1, 0) + jnp.where(has_right, 1, 0)
+    peers = 2 + 2 * ((xl + core) % 2) + jnp.where(has_left, 1, 0) + jnp.where(has_right, 1, 0)
     pl.semaphore_wait(barrier, peers)
 
     swap_h = [
         remote(stage_h.at[n], h_right.at[n], send_sem.at[n], h_sem.at[n], partner_id) for n in range(STEPS)
     ]
-    swap_lab = remote(stage_lab, lab, send_sem.at[4], lab_sem, partner_id)
+    swap_lab = remote(stage_lab, lab, send_sem.at[4], lab_sem, other_id)
     swap_u = remote(stage_u, u.at[0, :, inner, :], send_sem.at[5], u_sem.at[0], partner_id)
     swap_guess = remote(guess.at[xl, 0], guess_right, send_sem.at[6], gr_sem, partner_id)
     pass_guess = remote(guess_right, guess_left, send_sem.at[7], gl_sem, right_id)
@@ -162,12 +174,14 @@
     @pl.when(swapped)
     def _():
         pass_on[0].wait()
-        for copy in swap_h:
-            copy.start()
+        swap_h[0].start()
         pass_on[1].wait()
         swap_lab.start()
         pass_on[2].wait()
         swap_u.start()
+        pass_on[3].wait()
+        for copy in swap_h[1:]:
+            copy.start()
 
     @pl.when(jnp.logical_and(swapped, takes_guess))
     def _():
@@ -177,20 +191,44 @@
     def _():
         keep[0].wait()
 
-    for n in range(STEPS):
-        pl.when(swapped)(swap_h[n].wait_recv)
-        pl.when(has_right)(pass_h(n).start)
+    pl.when(swapped)(swap_h[0].wait_recv)
+    pl.when(has_right)(pass_h(0).start)
+
+    @pl.when(stays)
+    def _():
+        keep[3].wait()
+        for n in range(1, STEPS):
+            pl.when(has_right)(pass_h(n).start)
+
+    nothing = jnp.zeros((NY, NZ), F32)
 
     @pl.when(jnp.logical_not(has_right))
     def _():
-        h_right[...] = jnp.zeros((STEPS, NY, NZ), F32)
+        h_right[0] = nothing
+        pl.when(stays)(lambda: h_right.__setitem__(slice(1, STEPS), jnp.zeros((STEPS - 1, NY, NZ), F32)))
 
     @pl.when(jnp.logical_not(has_left))
     def _():
         h_left[...] = jnp.zeros((STEPS, NY, NZ), F32)
+
+    def pass_next(n):
+        @pl.when(jnp.logical_and(swapped, n + 1 < STEPS))
+        def _():
+            follow = n + 1
+            remote(
+                stage_h.at[follow], h_right.at[follow], send_sem.at[follow], h_sem.at[follow], partner_id
+            ).wait_recv()
+            pl.when(has_right)(pass_h(follow).start)
+
+            @pl.when(jnp.logical_not(has_right))
+            def _():
+                h_right[follow] = nothing
 
     pl.when(stays)(keep[1].wait)
     pl.when(swapped)(swap_lab.wait_recv)
+
+    for copy in tables:
+        copy.wait()
 
     def pick(table, value):
         result = jnp.full(value.shape, table[0], F32)
@@ -281,6 +319,8 @@
             sweep(buf_b, state, rhs, co_d, flux)
             pl.when(has_right)(send_ql(tick, n).start)
             pl.when(has_left)(send_qf(tick, n).start)
+            if tick == 0:
+                pass_next(n)
             return carry
 
         lax.fori_loop(0, STEPS, dirichlet, 0)
@@ -380,7 +420,7 @@
     vm = lambda *shape: pltpu.VMEM(shape, F32)
     dma = lambda *shape: pltpu.SemaphoreType.DMA(shape)
     any_spec = pl.BlockSpec(memory_space=pl.ANY)
-    smem = pl.BlockSpec(memory_space=pltpu.SMEM)
+    hbm = pl.BlockSpec(memory_space=pltpu.HBM)
     per_step = (TICKS, STEPS) + plane
     return pl.pallas_call(
         kernel,
@@ -388,9 +428,11 @@
             jax.ShapeDtypeStruct((1, 2) + plane, F32),
             jax.ShapeDtypeStruct((1, 1, STEPS) + plane, F32),
         ),
-        in_specs=[smem, smem, any_spec, any_spec, any_spec, any_spec],
+        in_specs=[hbm] * 6,
         out_specs=(any_spec, any_spec),
         scratch_shapes=[
+            pltpu.SMEM((4,), F32),
+            pltpu.SMEM((4,), F32),
             pltpu.VMEM((2,) + plane, jnp.int32),
             vm(2, *plane),
             vm(STEPS, *plane),
@@ -426,14 +468,14 @@
             dma(TICKS, 2, STEPS),
             dma(TICKS, 2, STEPS),
             dma(STEPS + 1),
-            dma(3),
+            dma(6),
             dma(8 + TICKS + 1),
             dma(TICKS, 2, STEPS),
             dma(TICKS, 2, STEPS),
             dma(STEPS),
             dma(STEPS),
         ],
-        compiler_params=pltpu.CompilerParams(collective_id=0, has_side_effects=True),
+        compiler_params=pltpu.CompilerParams(collective_id=0, has_side_effects=True, vmem_limit_bytes=24 * 2**20),
     )(cond_table, cap_table, fields, labels, traces, new_guess)
 
 

time: 50.3 us -> 54.2 us (1.078)
  the two profiles are of different devices: /device:TPU:24 before, /device:TPU:25 now
where the time goes in v2:
time: 54.2 us; the launch traced here: 54 us
  Pallas kernels  46.9 us (87%)
  local copies, waits for them, and re-layouts  6.46 us (12%)
  between operations  0.65 us (1%)
    pallas_call x1, Pallas kernels, local(): pl.pallas_call(kernel, out_shape=(jax.ShapeDtypeStruct((1, 2) + plane, F3...  46.9 us
    unnamed x14, local copies, waits for them, and re-layouts  6.46 us

profile of v2, /device:TPU:25, one launch (start us, length us, event | category | flops | bytes accessed | tf_op | source)
XLA Modules:
  0.0 54.0 jit_solution(12780316115881262751)
XLA Ops:
  0.6 0.0 copy-start
  0.6 1.0 %copy-done = f32[2,1,4,128,128]{4,3,2,1,0:T(8,128)S(1)} copy-done((f32[2,1,4,128,128]{4,3,2,1,0:T(8,128)S(1)}, f32[2,1,4,128,128]{4,3,2,1,0:T(8,128)}, u32[]{:S(2)}) %copy-start) | copy-done | bytes 524312
  1.7 0.0 copy-start.1
  1.7 0.9 %copy-done.1 = f32[1,1,4,128,128]{4,3,2,1,0:T(8,128)S(1)} copy-done((f32[1,1,4,128,128]{4,3,2,1,0:T(8,128)S(1)}, f32[1,1,4,128,128]{4,3,2,1,0:T(8,128)}, u32[]{:S(2)}) %copy-start.1) | copy-done | bytes 262168
  2.6 0.0 copy-start.2
  2.6 0.9 %copy-done.2 = f32[1,2,128,128]{3,2,1,0:T(8,128)S(1)} copy-done((f32[1,2,128,128]{3,2,1,0:T(8,128)S(1)}, f32[1,2,128,128]{3,2,1,0:T(8,128)}, u32[]{:S(2)}) %copy-start.2) | copy-done | bytes 131096
  3.5 0.0 copy-start.3
  3.5 0.9 %copy-done.3 = s32[2,128,128]{2,1,0:T(8,128)S(1)} copy-done((s32[2,128,128]{2,1,0:T(8,128)S(1)}, s32[2,128,128]{2,1,0:T(8,128)}, u32[]{:S(2)}) %copy-start.3) | copy-done | bytes 131096
  4.4 0.0 copy-start.4
  4.4 0.7 %copy-done.4 = f32[4]{0:T(128)S(1)} copy-done((f32[4]{0:T(128)S(1)}, f32[4]{0:T(128)}, u32[]{:S(2)}) %copy-start.4) | copy-done | bytes 40
  5.1 0.0 copy-start.5
  5.1 0.7 %copy-done.5 = f32[4]{0:T(128)S(1)} copy-done((f32[4]{0:T(128)S(1)}, f32[4]{0:T(128)}, u32[]{:S(2)}) %copy-start.5) | copy-done | bytes 40
  5.7 46.9 %shard_map.77 = (f32[1,2,128,128]{3,2,1,0:T(8,128)S(1)}, f32[1,1,4,128,128]{4,3,2,1,0:T(8,128)S(1)}) custom-call(f32[4]{0:T(128)S(1)} %copy-done.4, f32[4]{0:T(128)S(1)} %copy-done.5, f32[1,2,128,128]{3,2,1,0:T(8,128)S(1)} %copy-done.2, s32[2,128,128]{2,1,0:T(8,128)S(1)} %copy-done.3, f32[1,1,4,128,128]{4,3,2,1,0:T(8,128)S(1)} %copy-done.1, ...), custom_call_target="tpu_custom_call" | custom-call | tf_op jit(solution)/shard_map/pallas_call | solution.py:425
  52.6 0.7 %copy.10 = f32[1,2,128,128]{3,2,1,0:T(8,128)} copy(f32[1,2,128,128]{3,2,1,0:T(8,128)S(1)} %get-tuple-element.4) | data formatting | bytes 262144
  53.3 0.7 %copy.11 = f32[1,1,4,128,128]{4,3,2,1,0:T(8,128)} copy(f32[1,1,4,128,128]{4,3,2,1,0:T(8,128)S(1)} %get-tuple-element.5) | data formatting | bytes 524288
Async XLA Ops:
  0.6 1.0 %copy-start = (f32[2,1,4,128,128]{4,3,2,1,0:T(8,128)S(1)}, f32[2,1,4,128,128]{4,3,2,1,0:T(8,128)}, u32[]{:S(2)}) copy-start(f32[2,1,4,128,128]{4,3,2,1,0:T(8,128)} %guess.1) | copy-start | bytes 1572868
  1.7 0.9 %copy-start.1 = (f32[1,1,4,128,128]{4,3,2,1,0:T(8,128)S(1)}, f32[1,1,4,128,128]{4,3,2,1,0:T(8,128)}, u32[]{:S(2)}) copy-start(f32[1,1,4,128,128]{4,3,2,1,0:T(8,128)} %traces.1) | copy-start | bytes 786436
  2.6 0.9 %copy-start.2 = (f32[1,2,128,128]{3,2,1,0:T(8,128)S(1)}, f32[1,2,128,128]{3,2,1,0:T(8,128)}, u32[]{:S(2)}) copy-start(f32[1,2,128,128]{3,2,1,0:T(8,128)} %fields.1) | copy-start | bytes 393220
  3.5 0.9 %copy-start.3 = (s32[2,128,128]{2,1,0:T(8,128)S(1)}, s32[2,128,128]{2,1,0:T(8,128)}, u32[]{:S(2)}) copy-start(s32[2,128,128]{2,1,0:T(8,128)} %labels.1) | copy-start | bytes 393220
  4.4 0.7 %copy-start.4 = (f32[4]{0:T(128)S(1)}, f32[4]{0:T(128)}, u32[]{:S(2)}) copy-start(f32[4]{0:T(128)} %cond_hbm.1) | copy-start | bytes 52
  5.1 0.7 %copy-start.5 = (f32[4]{0:T(128)S(1)}, f32[4]{0:T(128)}, u32[]{:S(2)}) copy-start(f32[4]{0:T(128)} %cap_hbm.1) | copy-start | bytes 52

commit v3 on v2

--- a/solution.py
+++ b/solution.py
@@ -15,6 +15,7 @@
 PAD = 8
 ROWS = NY + 2 * PAD
 CHUNK = 32
+SPAN = 8
 F32 = jnp.float32
 
 
@@ -45,9 +46,11 @@
     cond_ref, cap_ref,
     stage_lab, stage_u, stage_h, lab, u, h_right, h_left, guess_right, guess_left,
     psi, buf_a, buf_b, rhs, co_d, co_n, end, inv_n,
-    qf, ql, q_left, q_right, pf, plast, p_left, p_right, back,
+    qs, qr, ps, pr, back,
+    lab_o, co_o, inv_o, psi_o, jump_in, jump_far,
     lab_sem, u_sem, h_sem, hl_sem, gr_sem, gl_sem,
     q_sem, p_sem, out_sem, load_sem, send_sem, qs_sem, ps_sem, hs_sem, bs_sem,
+    lab_o_sem, far_sem, in_sem,
 ):
     sub = lax.axis_index("sub")
     it = lax.axis_index("iter")
@@ -64,6 +67,23 @@
     stays = xl == core
     takes_guess = xh == 1
 
+    outer_right = jnp.logical_and(jnp.logical_and(core == 1, has_right), pair % SPAN == SPAN - 1)
+    outer_left = jnp.logical_and(jnp.logical_and(core == 0, has_left), pair % SPAN == 0)
+    long = jnp.logical_or(outer_right, outer_left)
+    short = jnp.logical_not(long)
+    exists = (has_left, has_right)
+    restart = [None] + [ring == 4 - tick for tick in range(1, TICKS)]
+    useful = [ring != 3 - tick for tick in range(TICKS - 1)] + [ring >= 0]
+    q_wait = (
+        jnp.logical_and(has_left, jnp.logical_not(outer_right)),
+        jnp.logical_and(has_right, jnp.logical_not(outer_left)),
+    )
+    p_uses = (
+        jnp.logical_and(has_left, jnp.logical_not(outer_left)),
+        jnp.logical_and(has_right, jnp.logical_not(outer_right)),
+    )
+    outer_id = {"sub": sub + 4 * core - 2, "iter": it + 1 - 2 * core}
+
     right_id = {"sub": sub + 2 * core, "iter": it + 1 - 2 * core}
     left_id = {"sub": sub - 2 * (1 - core), "iter": it + 1 - 2 * core}
     partner_id = {"sub": sub + 1 - 2 * xl, "iter": it + 1 - 2 * core}
@@ -85,7 +105,7 @@
     inner = pl.ds(PAD, NY)
 
     zero_pad = jnp.zeros((2, PAD, NZ), F32)
-    for ref in (buf_a, buf_b, psi):
+    for ref in (buf_a, buf_b, psi, psi_o):
         ref[:, 0:PAD, :] = zero_pad
         ref[:, PAD + NY : ROWS, :] = zero_pad
     for tick in range(TICKS):
@@ -156,17 +176,24 @@
     def pass_h(n):
         return remote(h_right.at[n], h_left.at[n], hs_sem.at[n], hl_sem.at[n], right_id)
 
-    def send_qf(t, n):
-        return remote(qf.at[t, n], q_right.at[t, n], qs_sem.at[t, 0, n], q_sem.at[t, 1, n], left_id)
-
-    def send_ql(t, n):
-        return remote(ql.at[t, n], q_left.at[t, n], qs_sem.at[t, 1, n], q_sem.at[t, 0, n], right_id)
-
-    def send_pf(t, n):
-        return remote(pf.at[t, n], p_right.at[t, n], ps_sem.at[t, 0, n], p_sem.at[t, 1, n], left_id)
-
-    def send_pl(t, n):
-        return remote(plast.at[t, n], p_left.at[t, n], ps_sem.at[t, 1, n], p_sem.at[t, 0, n], right_id)
+    sides = (left_id, right_id)
+
+    def send_q(side, t, n):
+        return remote(qs.at[side, t, n], qr.at[1 - side, t, n], qs_sem.at[t, side, n], q_sem.at[t, 1 - side, n], sides[side])
+
+    def send_p(side, t, n):
+        return remote(ps.at[side, t, n], pr.at[1 - side, t, n], ps_sem.at[t, side, n], p_sem.at[t, 1 - side, n], sides[side])
+
+    def got_q(side, t, n):
+        return remote(qs.at[side, t, n], qr.at[side, t, n], qs_sem.at[t, side, n], q_sem.at[t, side, n], left_id)
+
+    def got_p(side, t, n):
+        return remote(ps.at[side, t, n], pr.at[side, t, n], ps_sem.at[t, side, n], p_sem.at[t, side, n], left_id)
+
+    def send_jump(t, n):
+        return remote(jump_in.at[t, n], jump_far.at[t, n], in_sem.at[t, n], far_sem.at[t, n], outer_id)
+
+    send_lab = remote(lab, lab_o, send_sem.at[8 + TICKS + 1], lab_o_sem, outer_id)
 
     def send_home(n):
         return remote(back.at[n], out_h.at[0, 0, n], bs_sem.at[n], out_sem.at[n], home_id)
@@ -200,6 +227,11 @@
         for n in range(1, STEPS):
             pl.when(has_right)(pass_h(n).start)
 
+        @pl.when(takes_guess)
+        def _():
+            keep_guess.wait()
+            pl.when(has_right)(pass_guess.start)
+
     nothing = jnp.zeros((NY, NZ), F32)
 
     @pl.when(jnp.logical_not(has_right))
@@ -211,18 +243,16 @@
     def _():
         h_left[...] = jnp.zeros((STEPS, NY, NZ), F32)
 
-    def pass_next(n):
-        @pl.when(jnp.logical_and(swapped, n + 1 < STEPS))
+    def pass_rest(n):
+        @pl.when(jnp.logical_and(swapped, n == 0))
         def _():
-            follow = n + 1
-            remote(
-                stage_h.at[follow], h_right.at[follow], send_sem.at[follow], h_sem.at[follow], partner_id
-            ).wait_recv()
-            pl.when(has_right)(pass_h(follow).start)
+            for follow in range(1, STEPS):
+                swap_h[follow].wait_recv()
+                pl.when(has_right)(pass_h(follow).start)
 
             @pl.when(jnp.logical_not(has_right))
             def _():
-                h_right[follow] = nothing
+                h_right[1:STEPS] = jnp.zeros((STEPS - 1, NY, NZ), F32)
 
     pl.when(stays)(keep[1].wait)
     pl.when(swapped)(swap_lab.wait_recv)
@@ -236,70 +266,111 @@
             result = jnp.where(value == cls, table[cls], result)
         return result
 
-    for plane in range(2):
-        for row in range(0, NY, CHUNK):
-            buf_a[plane, PAD + row : PAD + row + CHUNK, :] = pick(cond_ref, lab[plane, row : row + CHUNK, :])
+    pl.when(long)(send_lab.start)
     lane = lax.broadcasted_iota(jnp.int32, (CHUNK, NZ), 1)
     line = lax.broadcasted_iota(jnp.int32, (CHUNK, NZ), 0)
-    for plane in range(2):
-        edge = has_left if plane == 0 else has_right
+
+    def coefficients(label, scratch, edges, own):
+        for plane in range(2):
+            for row in range(0, NY, CHUNK):
+                scratch[plane, PAD + row : PAD + row + CHUNK, :] = pick(cond_ref, label[plane, row : row + CHUNK, :])
+        for plane in range(2):
+            for row in range(0, NY, CHUNK):
+                here = slice(row, row + CHUNK)
+                base = PAD + row
+                k = scratch[plane, base : base + CHUNK, :]
+                twice = 2.0 * k
+                face_x = harmonic(k, scratch[1 - plane, base : base + CHUNK, :])
+                face_u = harmonic(k, scratch[plane, base - 1 : base - 1 + CHUNK, :])
+                face_d = harmonic(k, scratch[plane, base + 1 : base + 1 + CHUNK, :])
+                face_l = jnp.where(lane == 0, 0.0, harmonic(k, pltpu.roll(k, 1, 1)))
+                face_r = jnp.where(lane == NZ - 1, 0.0, harmonic(k, pltpu.roll(k, NZ - 1, 1)))
+                side_u = jnp.where(line + row == 0, twice, face_u) if row == 0 else face_u
+                side_d = jnp.where(line + row == NY - 1, twice, face_d) if row + CHUNK == NY else face_d
+                side_l = jnp.where(lane == 0, twice, face_l)
+                side_r = jnp.where(lane == NZ - 1, twice, face_r)
+                capacity = pick(cap_ref, label[plane, here, :])
+                common = capacity + face_x + side_u + side_d + side_l + side_r
+                faces = (face_x, face_u, face_d, face_l, face_r, capacity)
+                if own:
+                    inv_neu = 1.0 / jnp.where(edges[plane], common, common + twice)
+                    inv_dir = 1.0 / (common + twice)
+                    for j, face in enumerate(faces):
+                        co_d[j, plane, here, :] = face * inv_dir
+                    co_d[6, plane, here, :] = twice * inv_dir
+                    end[plane, here, :] = twice
+                else:
+                    inv_neu = 1.0 / common
+                for j, face in enumerate(faces):
+                    (co_n if own else co_o)[j, plane, here, :] = face * inv_neu
+                (inv_n if own else inv_o)[plane, here, :] = inv_neu
+
+    coefficients(lab, buf_a, exists, True)
+
+    pl.when(stays)(keep[2].wait)
+    pl.when(swapped)(swap_u.wait_recv)
+
+    last = TICKS - 1
+
+    def inner_jump(t, n, carry):
+        got_q(1 - core, t, n).wait_recv()
         for row in range(0, NY, CHUNK):
             here = slice(row, row + CHUNK)
-            base = PAD + row
-            k = buf_a[plane, base : base + CHUNK, :]
-            twice = 2.0 * k
-            face_x = harmonic(k, buf_a[1 - plane, base : base + CHUNK, :])
-            face_u = harmonic(k, buf_a[plane, base - 1 : base - 1 + CHUNK, :])
-            face_d = harmonic(k, buf_a[plane, base + 1 : base + 1 + CHUNK, :])
-            face_l = jnp.where(lane == 0, 0.0, harmonic(k, pltpu.roll(k, 1, 1)))
-            face_r = jnp.where(lane == NZ - 1, 0.0, harmonic(k, pltpu.roll(k, NZ - 1, 1)))
-            side_u = jnp.where(line + row == 0, twice, face_u) if row == 0 else face_u
-            side_d = jnp.where(line + row == NY - 1, twice, face_d) if row + CHUNK == NY else face_d
-            side_l = jnp.where(lane == 0, twice, face_l)
-            side_r = jnp.where(lane == NZ - 1, twice, face_r)
-            capacity = pick(cap_ref, lab[plane, here, :])
-            common = capacity + face_x + side_u + side_d + side_l + side_r
-            inv_dir = 1.0 / (common + twice)
-            inv_neu = 1.0 / jnp.where(edge, common, common + twice)
-            faces = (face_x, face_u, face_d, face_l, face_r, capacity)
-            for j, face in enumerate(faces):
-                co_d[j, plane, here, :] = face * inv_dir
-                co_n[j, plane, here, :] = face * inv_neu
-            co_d[6, plane, here, :] = twice * inv_dir
-            end[plane, here, :] = twice
-            inv_n[plane, here, :] = inv_neu
-
-    pl.when(stays)(keep[2].wait)
-    pl.when(swapped)(swap_u.wait_recv)
+            jump_in[t, n, here, :] = qs[1 - core, t, n, here, :] + qr[1 - core, t, n, here, :]
+        if t < last:
+            send_jump(t, n).start()
+        else:
+            pl.when(outer_left)(send_jump(t, n).start)
+        return carry
+
+    def outer(t, n):
+        send_jump(t, n).wait_recv()
+        near, far = 1 - core, core
+        for row in range(0, NY, CHUNK):
+            here = slice(row, row + CHUNK)
+            rows = slice(PAD + row, PAD + row + CHUNK)
+            jump = qs[core, t, n, here, :] + qr[core, t, n, here, :]
+            rhs[near, here, :] = inv_o[near, here, :] * jump + co_o[5, near, here, :] * psi_o[near, rows, :]
+            rhs[far, here, :] = (
+                inv_o[far, here, :] * jump_far[t, n, here, :] + co_o[5, far, here, :] * psi_o[far, rows, :]
+            )
+        sweep(psi_o, buf_a, rhs, co_o)
+        sweep(buf_a, buf_b, rhs, co_o)
+        sweep(buf_b, psi_o, rhs, co_o)
+        for row in range(0, NY, CHUNK):
+            pr[core, t, n, row : row + CHUNK, :] = psi_o[near, PAD + row : PAD + row + CHUNK, :]
 
     for tick in range(TICKS):
         state = u.at[tick]
         if tick > 0:
-            restart = ring == (4 - tick)
-            restart_r = jnp.logical_and(restart, has_right)
-            restart_l = jnp.logical_and(restart, has_left)
             move_u[tick - 1].wait_recv()
-            if tick == 1:
-                pl.when(jnp.logical_and(takes_guess, has_left))(pass_guess.wait_recv)
+            pl.when(jnp.logical_and(restart[tick], has_left))(pass_guess.wait_recv)
 
         def dirichlet(n, carry, tick=tick, state=state):
             if tick == 0:
                 pl.when(has_left)(pass_h(n).wait_recv)
             else:
-                pl.when(has_right)(send_pf(tick - 1, n).wait_recv)
-                pl.when(has_left)(send_pl(tick - 1, n).wait_recv)
                 if tick == 1:
                     pl.when(has_right)(pass_h(n).wait_send)
-                for row in range(0, NY, CHUNK):
-                    here = slice(row, row + CHUNK)
-                    old = h_right[n, here, :]
-                    new = old + 0.25 * (plast[tick - 1, n, here, :] + p_right[tick - 1, n, here, :])
-                    new = jnp.where(has_right, new, 0.0)
-                    h_right[n, here, :] = jnp.where(restart_r, guess_right[n, here, :], new)
-                    old = h_left[n, here, :]
-                    new = old + 0.25 * (p_left[tick - 1, n, here, :] + pf[tick - 1, n, here, :])
-                    new = jnp.where(has_left, new, 0.0)
-                    h_left[n, here, :] = jnp.where(restart_l, guess_left[n, here, :], new)
+
+                @pl.when(useful[tick - 1])
+                def _():
+                    pl.when(long)(lambda: outer(tick - 1, n))
+                    for side, trace in enumerate((h_left, h_right)):
+                        pl.when(p_uses[side])(got_p(side, tick - 1, n).wait_recv)
+                        for row in range(0, NY, CHUNK):
+                            here = slice(row, row + CHUNK)
+                            both = ps[side, tick - 1, n, here, :] + pr[side, tick - 1, n, here, :]
+                            new = trace[n, here, :] + 0.25 * both
+                            trace[n, here, :] = jnp.where(exists[side], new, 0.0)
+
+                @pl.when(restart[tick])
+                def _():
+                    for side, (trace, taken) in enumerate(((h_left, guess_left), (h_right, guess_right))):
+                        for row in range(0, NY, CHUNK):
+                            here = slice(row, row + CHUNK)
+                            trace[n, here, :] = jnp.where(exists[side], taken[n, here, :], 0.0)
+
             for plane, trace in enumerate((h_left, h_right)):
                 for row in range(0, NY, CHUNK):
                     here = slice(row, row + CHUNK)
@@ -309,18 +380,16 @@
                     )
 
             def flux(plane, here, value):
-                if plane == 0:
-                    qf[tick, n, here, :] = end[0, here, :] * (value - h_left[n, here, :])
-                else:
-                    ql[tick, n, here, :] = end[1, here, :] * (value - h_right[n, here, :])
+                trace = (h_left, h_right)[plane]
+                qs[plane, tick, n, here, :] = end[plane, here, :] * (value - trace[n, here, :])
 
             sweep(state, buf_a, rhs, co_d)
             sweep(buf_a, buf_b, rhs, co_d)
             sweep(buf_b, state, rhs, co_d, flux)
-            pl.when(has_right)(send_ql(tick, n).start)
-            pl.when(has_left)(send_qf(tick, n).start)
+            pl.when(jnp.logical_and(has_right, useful[tick]))(send_q(1, tick, n).start)
+            pl.when(jnp.logical_and(has_left, useful[tick]))(send_q(0, tick, n).start)
             if tick == 0:
-                pass_next(n)
+                pass_rest(n)
             return carry
 
         lax.fori_loop(0, STEPS, dirichlet, 0)
@@ -328,23 +397,33 @@
             move_u[tick].start()
         else:
             home_u.start()
+        if tick + 1 < TICKS:
+
+            @pl.when(jnp.logical_and(swapped, restart[tick + 1]))
+            def _():
+                swap_guess.wait_recv()
+                pl.when(has_right)(pass_guess.start)
+
         if tick == 0:
 
-            @pl.when(takes_guess)
+            @pl.when(long)
             def _():
-                pl.when(stays)(keep_guess.wait)
-                pl.when(swapped)(swap_guess.wait_recv)
-                pl.when(has_right)(pass_guess.start)
+                send_lab.wait_recv()
+                coefficients(lab_o, psi_o, None, False)
+
+        @pl.when(jnp.logical_and(long, useful[tick]))
+        def _():
+            lax.fori_loop(0, STEPS, functools.partial(inner_jump, tick), 0)
+            psi_o[:, PAD : PAD + NY, :] = jnp.zeros((2, NY, NZ), F32)
 
         def neumann(n, carry, tick=tick, first=False):
-            pl.when(has_right)(send_qf(tick, n).wait_recv)
-            pl.when(has_left)(send_ql(tick, n).wait_recv)
+            for side in range(2):
+                pl.when(q_wait[side])(got_q(side, tick, n).wait_recv)
             for plane in range(2):
-                own, got, edge = ((qf, q_left, has_left), (ql, q_right, has_right))[plane]
                 for row in range(0, NY, CHUNK):
                     here = slice(row, row + CHUNK)
-                    jump = own[tick, n, here, :] + got[tick, n, here, :]
-                    value = inv_n[plane, here, :] * jnp.where(edge, jump, 0.0)
+                    jump = qs[plane, tick, n, here, :] + qr[plane, tick, n, here, :]
+                    value = inv_n[plane, here, :] * jnp.where(exists[plane], jump, 0.0)
                     if not first:
                         value = value + co_n[5, plane, here, :] * psi[plane, PAD + row : PAD + row + CHUNK, :]
                     rhs[plane, here, :] = value
@@ -352,27 +431,29 @@
                         buf_a[plane, PAD + row : PAD + row + CHUNK, :] = value
 
             def ends(plane, here, value):
-                (pf, plast)[plane][tick, n, here, :] = value
+                ps[plane, tick, n, here, :] = value
 
             if not first:
                 sweep(psi, buf_a, rhs, co_n)
             sweep(buf_a, buf_b, rhs, co_n)
             sweep(buf_b, psi, rhs, co_n, ends)
-            pl.when(has_left)(send_pf(tick, n).start)
+            pl.when(p_uses[0])(send_p(0, tick, n).start)
             if tick + 1 < TICKS:
-                pl.when(has_right)(send_pl(tick, n).start)
+                pl.when(p_uses[1])(send_p(1, tick, n).start)
             return carry
 
-        neumann(0, 0, first=True)
-        lax.fori_loop(1, STEPS, neumann, 0)
-
-    last = TICKS - 1
+        @pl.when(useful[tick])
+        def _():
+            neumann(0, 0, first=True)
+            lax.fori_loop(1, STEPS, neumann, 0)
+
 
     def finish(n, carry):
-        pl.when(has_right)(send_pf(last, n).wait_recv)
+        pl.when(outer_right)(lambda: outer(last, n))
+        pl.when(p_uses[1])(got_p(1, last, n).wait_recv)
         for row in range(0, NY, CHUNK):
             here = slice(row, row + CHUNK)
-            new = h_right[n, here, :] + 0.25 * (plast[last, n, here, :] + p_right[last, n, here, :])
+            new = h_right[n, here, :] + 0.25 * (ps[1, last, n, here, :] + pr[1, last, n, here, :])
             back[n, here, :] = jnp.where(has_right, new, 0.0)
         send_home(n).start()
         return carry
@@ -392,26 +473,51 @@
         copy.wait_send()
     home_u.wait_send()
 
-    @pl.when(has_right)
-    def _():
+    for side in range(2):
+
+        @pl.when(exists[side])
+        def _():
+            for n in range(STEPS):
+                for t in range(TICKS):
+                    pl.when(useful[t])(send_q(side, t, n).wait_send)
+
+        @pl.when(p_uses[side])
+        def _():
+            for n in range(STEPS):
+                for t in range(TICKS if side == 0 else last):
+                    pl.when(useful[t])(send_p(side, t, n).wait_send)
+
+    @pl.when(long)
+    def _():
+        send_lab.wait_send()
         for n in range(STEPS):
-            for t in range(TICKS):
-                send_ql(t, n).wait_send()
-                if t < last:
-                    send_pl(t, n).wait_send()
-
-    @pl.when(has_left)
+            for t in range(last):
+                pl.when(useful[t])(send_jump(t, n).wait_send)
+
+    @pl.when(outer_left)
     def _():
         for n in range(STEPS):
-            for t in range(TICKS):
-                send_qf(t, n).wait_send()
-                send_pf(t, n).wait_send()
+            send_jump(last, n).wait_send()
 
     for n in range(STEPS):
         send_home(n).wait_send()
     home_u.wait_recv()
     for n in range(STEPS):
         send_home(n).wait_recv()
+
+
+def deliver(field, trace, out_field, out_trace, block, in_sem, out_sem):
+    pieces = [(field.at[0, i], out_field.at[0, i]) for i in range(2)]
+    pieces += [(trace.at[0, 0, n], out_trace.at[0, 0, n]) for n in range(STEPS)]
+    loads = [pltpu.make_async_copy(src, block.at[i], in_sem.at[i]) for i, (src, _) in enumerate(pieces)]
+    stores = [pltpu.make_async_copy(block.at[i], dst, out_sem.at[i]) for i, (_, dst) in enumerate(pieces)]
+    for copy in loads:
+        copy.start()
+    for load, store in zip(loads, stores):
+        load.wait()
+        store.start()
+    for store in stores:
+        store.wait()
 
 
 def local(fields, labels, traces, new_guess, cond_table, cap_table):
@@ -422,7 +528,7 @@
     any_spec = pl.BlockSpec(memory_space=pl.ANY)
     hbm = pl.BlockSpec(memory_space=pltpu.HBM)
     per_step = (TICKS, STEPS) + plane
-    return pl.pallas_call(
+    results = pl.pallas_call(
         kernel,
         out_shape=(
             jax.ShapeDtypeStruct((1, 2) + plane, F32),
@@ -450,15 +556,17 @@
             vm(6, 2, *plane),
             vm(2, *plane),
             vm(2, *plane),
+            vm(2, *per_step),
+            vm(2, *per_step),
+            vm(2, *per_step),
+            vm(2, *per_step),
+            vm(STEPS, *plane),
+            pltpu.VMEM((2,) + plane, jnp.int32),
+            vm(6, 2, *plane),
+            vm(2, *plane),
+            vm(*field),
             vm(*per_step),
             vm(*per_step),
-            vm(*per_step),
-            vm(*per_step),
-            vm(*per_step),
-            vm(*per_step),
-            vm(*per_step),
-            vm(*per_step),
-            vm(STEPS, *plane),
             pltpu.SemaphoreType.DMA,
             dma(TICKS),
             dma(STEPS),
@@ -469,14 +577,27 @@
             dma(TICKS, 2, STEPS),
             dma(STEPS + 1),
             dma(6),
-            dma(8 + TICKS + 1),
+            dma(8 + TICKS + 2),
             dma(TICKS, 2, STEPS),
             dma(TICKS, 2, STEPS),
             dma(STEPS),
             dma(STEPS),
+            pltpu.SemaphoreType.DMA,
+            dma(TICKS, STEPS),
+            dma(TICKS, STEPS),
         ],
-        compiler_params=pltpu.CompilerParams(collective_id=0, has_side_effects=True, vmem_limit_bytes=24 * 2**20),
+        compiler_params=pltpu.CompilerParams(collective_id=0, has_side_effects=True),
     )(cond_table, cap_table, fields, labels, traces, new_guess)
+    return pl.pallas_call(
+        deliver,
+        out_shape=(
+            jax.ShapeDtypeStruct((1, 2) + plane, F32),
+            jax.ShapeDtypeStruct((1, 1, STEPS) + plane, F32),
+        ),
+        in_specs=[any_spec] * 2,
+        out_specs=(any_spec, any_spec),
+        scratch_shapes=[vm(2 + STEPS, *plane), dma(2 + STEPS), dma(2 + STEPS)],
+    )(*results)
 
 
 def solution(mesh):

time: 54.2 us -> 47.3 us (0.87)
  local copies, waits for them, and re-layouts: 6.46 us -> 0 us
    unnamed x14 -> x0, local copies, waits for them, and re-layouts: 6.46 us -> none
    pallas_call x1, Pallas kernels: 46.9 us -> 44.7 us  [local(): pl.pallas_call(kernel, out_shape=(jax.ShapeDtypeStruct((1, 2) + plane, F3...]
    pallas_call x0 -> x1, Pallas kernels: none -> 1.73 us  [local(): pl.pallas_call(deliver, out_shape=(jax.ShapeDtypeStruct((1, 2) + plane, F...]
where the time goes in v3:
time: 47.3 us; the launch traced here: 47.1 us
  Pallas kernels  46.5 us (98%)
  between operations  0.64 us (1%)
    pallas_call x1, Pallas kernels, local(): pl.pallas_call(kernel, out_shape=(jax.ShapeDtypeStruct((1, 2) + plane, F3...  44.7 us
    pallas_call x1, Pallas kernels, local(): pl.pallas_call(deliver, out_shape=(jax.ShapeDtypeStruct((1, 2) + plane, F...  1.73 us

profile of v3, /device:TPU:25, one launch (start us, length us, event | category | flops | bytes accessed | tf_op | source)
XLA Modules:
  0.0 47.1 jit_solution(15751282873087115524)
XLA Ops:
  0.6 44.7 %shard_map.77 = (f32[1,2,128,128]{3,2,1,0:T(8,128)}, f32[1,1,4,128,128]{4,3,2,1,0:T(8,128)}) custom-call(f32[4]{0:T(128)} %cond_hbm.1, f32[4]{0:T(128)} %cap_hbm.1, f32[1,2,128,128]{3,2,1,0:T(8,128)} %fields.1, s32[2,128,128]{2,1,0:T(8,128)} %labels.1, f32[1,1,4,128,128]{4,3,2,1,0:T(8,128)} %traces.1, f32[2,1,4,128,128]{4,3,2,1,0:T(8,128)} %guess.1), custom_call_target="tpu_custom_call" | custom-call | tf_op jit(solution)/shard_map/pallas_call | solution.py:531
  45.4 1.7 %shard_map.78 = (f32[1,2,128,128]{3,2,1,0:T(8,128)}, f32[1,1,4,128,128]{4,3,2,1,0:T(8,128)}) custom-call(f32[1,2,128,128]{3,2,1,0:T(8,128)} %get-tuple-element.4.field, f32[1,1,4,128,128]{4,3,2,1,0:T(8,128)} %get-tuple-element.5.trace), custom_call_target="tpu_custom_call" | custom-call | tf_op jit(solution)/shard_map/pallas_call | solution.py:591

commit v4 on v3

--- a/solution.py
+++ b/solution.py
@@ -204,11 +204,11 @@
         swap_h[0].start()
         pass_on[1].wait()
         swap_lab.start()
-        pass_on[2].wait()
-        swap_u.start()
         pass_on[3].wait()
         for copy in swap_h[1:]:
             copy.start()
+        pass_on[2].wait()
+        swap_u.start()
 
     @pl.when(jnp.logical_and(swapped, takes_guess))
     def _():
@@ -217,42 +217,24 @@
     @pl.when(stays)
     def _():
         keep[0].wait()
-
-    pl.when(swapped)(swap_h[0].wait_recv)
-    pl.when(has_right)(pass_h(0).start)
-
-    @pl.when(stays)
-    def _():
         keep[3].wait()
-        for n in range(1, STEPS):
-            pl.when(has_right)(pass_h(n).start)
-
-        @pl.when(takes_guess)
-        def _():
-            keep_guess.wait()
-            pl.when(has_right)(pass_guess.start)
-
-    nothing = jnp.zeros((NY, NZ), F32)
+
+    for n in range(STEPS):
+        pl.when(swapped)(swap_h[n].wait_recv)
+        pl.when(has_right)(pass_h(n).start)
+
+    @pl.when(jnp.logical_and(stays, takes_guess))
+    def _():
+        keep_guess.wait()
+        pl.when(has_right)(pass_guess.start)
 
     @pl.when(jnp.logical_not(has_right))
     def _():
-        h_right[0] = nothing
-        pl.when(stays)(lambda: h_right.__setitem__(slice(1, STEPS), jnp.zeros((STEPS - 1, NY, NZ), F32)))
+        h_right[...] = jnp.zeros((STEPS, NY, NZ), F32)
 
     @pl.when(jnp.logical_not(has_left))
     def _():
         h_left[...] = jnp.zeros((STEPS, NY, NZ), F32)
-
-    def pass_rest(n):
-        @pl.when(jnp.logical_and(swapped, n == 0))
-        def _():
-            for follow in range(1, STEPS):
-                swap_h[follow].wait_recv()
-                pl.when(has_right)(pass_h(follow).start)
-
-            @pl.when(jnp.logical_not(has_right))
-            def _():
-                h_right[1:STEPS] = jnp.zeros((STEPS - 1, NY, NZ), F32)
 
     pl.when(stays)(keep[1].wait)
     pl.when(swapped)(swap_lab.wait_recv)
@@ -343,7 +325,6 @@
     for tick in range(TICKS):
         state = u.at[tick]
         if tick > 0:
-            move_u[tick - 1].wait_recv()
             pl.when(jnp.logical_and(restart[tick], has_left))(pass_guess.wait_recv)
 
         def dirichlet(n, carry, tick=tick, state=state):
@@ -371,6 +352,8 @@
                             here = slice(row, row + CHUNK)
                             trace[n, here, :] = jnp.where(exists[side], taken[n, here, :], 0.0)
 
+                pl.when(n == 0)(move_u[tick - 1].wait_recv)
+
             for plane, trace in enumerate((h_left, h_right)):
                 for row in range(0, NY, CHUNK):
                     here = slice(row, row + CHUNK)
@@ -388,8 +371,6 @@
             sweep(buf_b, state, rhs, co_d, flux)
             pl.when(jnp.logical_and(has_right, useful[tick]))(send_q(1, tick, n).start)
             pl.when(jnp.logical_and(has_left, useful[tick]))(send_q(0, tick, n).start)
-            if tick == 0:
-                pass_rest(n)
             return carry
 
         lax.fori_loop(0, STEPS, dirichlet, 0)
@@ -404,17 +385,9 @@
                 swap_guess.wait_recv()
                 pl.when(has_right)(pass_guess.start)
 
-        if tick == 0:
-
-            @pl.when(long)
-            def _():
-                send_lab.wait_recv()
-                coefficients(lab_o, psi_o, None, False)
-
         @pl.when(jnp.logical_and(long, useful[tick]))
         def _():
             lax.fori_loop(0, STEPS, functools.partial(inner_jump, tick), 0)
-            psi_o[:, PAD : PAD + NY, :] = jnp.zeros((2, NY, NZ), F32)
 
         def neumann(n, carry, tick=tick, first=False):
             for side in range(2):
@@ -445,6 +418,16 @@
         @pl.when(useful[tick])
         def _():
             neumann(0, 0, first=True)
+
+        @pl.when(long)
+        def _():
+            if tick == 0:
+                send_lab.wait_recv()
+                coefficients(lab_o, psi_o, None, False)
+            psi_o[:, PAD : PAD + NY, :] = jnp.zeros((2, NY, NZ), F32)
+
+        @pl.when(useful[tick])
+        def _():
             lax.fori_loop(1, STEPS, neumann, 0)
 
 

time: 47.3 us -> 46.7 us (0.987)
  Pallas kernels: 46.5 us -> 45.9 us
    pallas_call x1, Pallas kernels: 44.7 us -> 44.2 us  [local(): pl.pallas_call(kernel, out_shape=(jax.ShapeDtypeStruct((1, 2) + plane, F3...]
where the time goes in v4:
time: 46.7 us; the launch traced here: 46.6 us
  Pallas kernels  45.9 us (98%)
  between operations  0.64 us (1%)
    pallas_call x1, Pallas kernels, local(): pl.pallas_call(kernel, out_shape=(jax.ShapeDtypeStruct((1, 2) + plane, F3...  44.2 us
    pallas_call x1, Pallas kernels, local(): pl.pallas_call(deliver, out_shape=(jax.ShapeDtypeStruct((1, 2) + plane, F...  1.73 us

profile of v4, /device:TPU:25, one launch (start us, length us, event | category | flops | bytes accessed | tf_op | source)
XLA Modules:
  0.0 46.6 jit_solution(14904274713839337528)
XLA Ops:
  0.6 44.2 %shard_map.77 = (f32[1,2,128,128]{3,2,1,0:T(8,128)}, f32[1,1,4,128,128]{4,3,2,1,0:T(8,128)}) custom-call(f32[4]{0:T(128)} %cond_hbm.1, f32[4]{0:T(128)} %cap_hbm.1, f32[1,2,128,128]{3,2,1,0:T(8,128)} %fields.1, s32[2,128,128]{2,1,0:T(8,128)} %labels.1, f32[1,1,4,128,128]{4,3,2,1,0:T(8,128)} %traces.1, f32[2,1,4,128,128]{4,3,2,1,0:T(8,128)} %guess.1), custom_call_target="tpu_custom_call" | custom-call | tf_op jit(solution)/shard_map/pallas_call | solution.py:514
  44.8 1.7 %shard_map.78 = (f32[1,2,128,128]{3,2,1,0:T(8,128)}, f32[1,1,4,128,128]{4,3,2,1,0:T(8,128)}) custom-call(f32[1,2,128,128]{3,2,1,0:T(8,128)} %get-tuple-element.4.field, f32[1,1,4,128,128]{4,3,2,1,0:T(8,128)} %get-tuple-element.5.trace), custom_call_target="tpu_custom_call" | custom-call | tf_op jit(solution)/shard_map/pallas_call | solution.py:574

commit v5 on v4

--- a/solution.py
+++ b/solution.py
@@ -322,6 +322,17 @@
         for row in range(0, NY, CHUNK):
             pr[core, t, n, row : row + CHUNK, :] = psi_o[near, PAD + row : PAD + row + CHUNK, :]
 
+    def finish(n, carry, solve=True):
+        if solve:
+            pl.when(outer_right)(lambda: outer(last, n))
+        pl.when(p_uses[1])(got_p(1, last, n).wait_recv)
+        for row in range(0, NY, CHUNK):
+            here = slice(row, row + CHUNK)
+            new = h_right[n, here, :] + 0.25 * (ps[1, last, n, here, :] + pr[1, last, n, here, :])
+            back[n, here, :] = jnp.where(has_right, new, 0.0)
+        send_home(n).start()
+        return carry
+
     for tick in range(TICKS):
         state = u.at[tick]
         if tick > 0:
@@ -413,6 +424,11 @@
             pl.when(p_uses[0])(send_p(0, tick, n).start)
             if tick + 1 < TICKS:
                 pl.when(p_uses[1])(send_p(1, tick, n).start)
+            elif not first:
+                @pl.when(core == 0)
+                def _():
+                    finish(n - 1, 0, False)
+
             return carry
 
         @pl.when(useful[tick])
@@ -431,17 +447,14 @@
             lax.fori_loop(1, STEPS, neumann, 0)
 
 
-    def finish(n, carry):
-        pl.when(outer_right)(lambda: outer(last, n))
-        pl.when(p_uses[1])(got_p(1, last, n).wait_recv)
-        for row in range(0, NY, CHUNK):
-            here = slice(row, row + CHUNK)
-            new = h_right[n, here, :] + 0.25 * (ps[1, last, n, here, :] + pr[1, last, n, here, :])
-            back[n, here, :] = jnp.where(has_right, new, 0.0)
-        send_home(n).start()
-        return carry
-
-    lax.fori_loop(0, STEPS, finish, 0)
+    @pl.when(core == 1)
+    def _():
+        lax.fori_loop(0, STEPS, finish, 0)
+
+    @pl.when(core == 0)
+    def _():
+        finish(STEPS - 1, 0, False)
+
 
     @pl.when(swapped)
     def _():

time: 46.7 us -> 46.5 us (level)
  no operation moved by 1% of the time
where the time goes in v5:
time: 46.5 us; the launch traced here: 46.3 us
  Pallas kernels  45.7 us (98%)
  between operations  0.64 us (1%)
    pallas_call x1, Pallas kernels, local(): pl.pallas_call(kernel, out_shape=(jax.ShapeDtypeStruct((1, 2) + plane, F3...  43.9 us
    pallas_call x1, Pallas kernels, local(): pl.pallas_call(deliver, out_shape=(jax.ShapeDtypeStruct((1, 2) + plane, F...  1.73 us

profile of v5, /device:TPU:25, one launch (start us, length us, event | category | flops | bytes accessed | tf_op | source)
XLA Modules:
  0.0 46.3 jit_solution(5062383031561816178)
XLA Ops:
  0.6 43.9 %shard_map.77 = (f32[1,2,128,128]{3,2,1,0:T(8,128)}, f32[1,1,4,128,128]{4,3,2,1,0:T(8,128)}) custom-call(f32[4]{0:T(128)} %cond_hbm.1, f32[4]{0:T(128)} %cap_hbm.1, f32[1,2,128,128]{3,2,1,0:T(8,128)} %fields.1, s32[2,128,128]{2,1,0:T(8,128)} %labels.1, f32[1,1,4,128,128]{4,3,2,1,0:T(8,128)} %traces.1, f32[2,1,4,128,128]{4,3,2,1,0:T(8,128)} %guess.1), custom_call_target="tpu_custom_call" | custom-call | tf_op jit(solution)/shard_map/pallas_call | solution.py:527
  44.6 1.7 %shard_map.78 = (f32[1,2,128,128]{3,2,1,0:T(8,128)}, f32[1,1,4,128,128]{4,3,2,1,0:T(8,128)}) custom-call(f32[1,2,128,128]{3,2,1,0:T(8,128)} %get-tuple-element.4.field, f32[1,1,4,128,128]{4,3,2,1,0:T(8,128)} %get-tuple-element.5.trace), custom_call_target="tpu_custom_call" | custom-call | tf_op jit(solution)/shard_map/pallas_call | solution.py:587

commit v6 on v5

--- a/solution.py
+++ b/solution.py
@@ -70,6 +70,7 @@
     outer_right = jnp.logical_and(jnp.logical_and(core == 1, has_right), pair % SPAN == SPAN - 1)
     outer_left = jnp.logical_and(jnp.logical_and(core == 0, has_left), pair % SPAN == 0)
     long = jnp.logical_or(outer_right, outer_left)
+    lagging = jnp.logical_and(core == 0, jnp.logical_not(outer_left))
     short = jnp.logical_not(long)
     exists = (has_left, has_right)
     restart = [None] + [ring == 4 - tick for tick in range(1, TICKS)]
@@ -424,10 +425,16 @@
             pl.when(p_uses[0])(send_p(0, tick, n).start)
             if tick + 1 < TICKS:
                 pl.when(p_uses[1])(send_p(1, tick, n).start)
-            elif not first:
-                @pl.when(core == 0)
+            else:
+                @pl.when(outer_left)
                 def _():
-                    finish(n - 1, 0, False)
+                    finish(n, 0, False)
+
+                if not first:
+
+                    @pl.when(lagging)
+                    def _():
+                        finish(n - 1, 0, False)
 
             return carry
 
@@ -451,7 +458,7 @@
     def _():
         lax.fori_loop(0, STEPS, finish, 0)
 
-    @pl.when(core == 0)
+    @pl.when(lagging)
     def _():
         finish(STEPS - 1, 0, False)
 

time: 46.5 us -> 46.5 us (level)
  no operation moved by 1% of the time
where the time goes in v6:
time: 46.5 us; the launch traced here: 46.3 us
  Pallas kernels  45.7 us (98%)
  between operations  0.64 us (1%)
    pallas_call x1, Pallas kernels, local(): pl.pallas_call(kernel, out_shape=(jax.ShapeDtypeStruct((1, 2) + plane, F3...  44 us
    pallas_call x1, Pallas kernels, local(): pl.pallas_call(deliver, out_shape=(jax.ShapeDtypeStruct((1, 2) + plane, F...  1.73 us

profile of v6, /device:TPU:25, one launch (start us, length us, event | category | flops | bytes accessed | tf_op | source)
XLA Modules:
  0.0 46.3 jit_solution(10960754478356756168)
XLA Ops:
  0.6 44.0 %shard_map.77 = (f32[1,2,128,128]{3,2,1,0:T(8,128)}, f32[1,1,4,128,128]{4,3,2,1,0:T(8,128)}) custom-call(f32[4]{0:T(128)} %cond_hbm.1, f32[4]{0:T(128)} %cap_hbm.1, f32[1,2,128,128]{3,2,1,0:T(8,128)} %fields.1, s32[2,128,128]{2,1,0:T(8,128)} %labels.1, f32[1,1,4,128,128]{4,3,2,1,0:T(8,128)} %traces.1, f32[2,1,4,128,128]{4,3,2,1,0:T(8,128)} %guess.1), custom_call_target="tpu_custom_call" | custom-call | tf_op jit(solution)/shard_map/pallas_call | solution.py:534
  44.6 1.7 %shard_map.78 = (f32[1,2,128,128]{3,2,1,0:T(8,128)}, f32[1,1,4,128,128]{4,3,2,1,0:T(8,128)}) custom-call(f32[1,2,128,128]{3,2,1,0:T(8,128)} %get-tuple-element.4.field, f32[1,1,4,128,128]{4,3,2,1,0:T(8,128)} %get-tuple-element.5.trace), custom_call_target="tpu_custom_call" | custom-call | tf_op jit(solution)/shard_map/pallas_call | solution.py:594
